TPU v7x, 32 devices: a whole 2x2x4 slice. The times are simulated.
32 devices in a mesh: dp: 4 (over y, core), ctx: 8 (over z, x).
Axes of the slice: x: 2, y: 2, z: 4, core: 2. Of those that a mesh axis runs over, the one named last changes fastest.
Arguments:
- text: bfloat16 [4, 2, 128, 2048], P('dp', None, None, 'ctx'), may hold values from -6 to 6
- src: int32 [4], replicated, may hold values from 0 to 3, each once
- lengths: int32 [4, 2], replicated, may hold values from 1 to 128
- kv_weight: bfloat16 [2048, 2, 8192], P('dp', None, 'ctx'), may hold values from -0.125 to 0.125
- queries: bfloat16 [4, 2048, 4096], P('dp', 'ctx'), may hold values from -160 to 160
- grad_out: bfloat16 [4, 2048, 4096], P('dp', 'ctx'), may hold values from -6 to 6
Outputs:
- attended: bfloat16 [4, 2048, 4096], P('dp', 'ctx')
- grad_queries: bfloat16 [4, 2048, 4096], P('dp', 'ctx')
- grad_weight: float32 [2048, 2, 8192], P('dp', None, 'ctx')
Inputs may be any that keep to these rules, and one draw needn't show every extreme that they name: `src`: each text sample is used by exactly one latent sample. `lengths`: tokens of an encoder output at or beyond its length are padding.
All inputs are finite; a program needn't handle non-finite values.
Results may differ from a plain program's by a relative error of at most 0.018.
The roundings to bfloat16 on the way count: a program that leaves them out, or rounds other values in their place, can miss the bound.
Values may be sent and summed in bfloat16 or wider, within the bound.
A program may use at most 128 MiB of HBM per device.

v0:
```python
import functools
import math

import jax
import jax.numpy as jnp
from jax import lax
from jax.experimental import pallas as pl
from jax.experimental.pallas import tpu as pltpu
from jax.sharding import PartitionSpec as P

HEAD = 128


def dot(a, b, dims):
    return lax.dot_general(a, b, (dims, ((), ())), preferred_element_type=jnp.float32)


def attend_block(block, bias_ref, q_ref, g_ref, kv_ref, out_ref, gq_ref, gkv_ref):
    scale = 1.0 / math.sqrt(HEAD)
    bias = bias_ref[...]
    heads = kv_ref.shape[2] // (2 * HEAD)
    for h in range(heads):
        own = pl.ds(pl.multiple_of((block * heads + h) * HEAD, HEAD), HEAD)
        at_key = slice(2 * h * HEAD, (2 * h + 1) * HEAD)
        at_value = slice((2 * h + 1) * HEAD, (2 * h + 2) * HEAD)
        q = q_ref[:, own]
        g = g_ref[:, own]
        key = kv_ref[block, :, at_key]
        value = kv_ref[block, :, at_value]
        scores = dot(q, key, ((1,), (1,))) * scale + bias
        top = jnp.max(scores, axis=-1, keepdims=True)
        weights = jnp.exp(scores - top)
        probs = weights * (1.0 / jnp.sum(weights, axis=-1, keepdims=True))
        probs_low = probs.astype(jnp.bfloat16)
        out_ref[:, own] = dot(probs_low, value, ((1,), (0,))).astype(jnp.bfloat16)
        grad_probs = dot(g, value, ((1,), (1,)))
        delta = jnp.sum(probs * grad_probs, axis=-1, keepdims=True)
        grad_scores = (probs * (grad_probs - delta) * scale).astype(jnp.bfloat16)
        gq_ref[:, own] = dot(grad_scores, key, ((1,), (0,))).astype(jnp.bfloat16)
        gkv_ref[block, :, at_key] = dot(grad_scores, q, ((0,), (0,))).astype(gkv_ref.dtype)
        gkv_ref[block, :, at_value] = dot(probs_low, g, ((0,), (0,))).astype(gkv_ref.dtype)


def greet(axis, a, last, up, down, partner):
    barrier = pltpu.get_barrier_semaphore()

    def hello(target):
        pl.semaphore_signal(barrier, inc=1, device_id={axis: target}, device_id_type=pl.DeviceIdType.MESH)

    hello(partner)

    @pl.when(a < last)
    def _():
        hello(up)

    @pl.when(a > 0)
    def _():
        hello(down)

    if last == 0:
        pl.semaphore_wait(barrier, 1)
    else:
        @pl.when((a > 0) & (a < last))
        def _():
            pl.semaphore_wait(barrier, 3)

        @pl.when((a == 0) | (a == last))
        def _():
            pl.semaphore_wait(barrier, 2)


def gather_kernel(axis, n, own_ref, out_ref, own_sem, send_sems, recv_sems):
    me = lax.axis_index(axis)
    a, b = me // 2, me % 2
    last = n // 2 - 1
    up, down, partner = me + 2, me - 2, a * 2 + (1 - b)
    greet(axis, a, last, up, down, partner)
    mine = pltpu.make_async_copy(own_ref, out_ref.at[me], own_sem)
    mine.start()

    def hop(source, block, way, target):
        return pltpu.make_async_remote_copy(
            src_ref=source, dst_ref=out_ref.at[block], send_sem=send_sems.at[block, way],
            recv_sem=recv_sems.at[block], device_id={axis: target}, device_id_type=pl.DeviceIdType.MESH,
        )

    @pl.when(a < last)
    def _():
        hop(own_ref, me, 0, up).start()

    @pl.when(a > 0)
    def _():
        hop(own_ref, me, 1, down).start()

    hop(own_ref, me, 2, partner).start()
    for s in range(1, last + 1):
        @pl.when(a >= s)
        def _():
            block = (a - s) * 2 + b
            hop(own_ref, block, 0, partner).wait_recv()

            @pl.when(a < last)
            def _():
                hop(out_ref.at[block], block, 0, up).start()

            hop(out_ref.at[block], block, 2, partner).start()

        @pl.when(a + s <= last)
        def _():
            block = (a + s) * 2 + b
            hop(own_ref, block, 1, partner).wait_recv()

            @pl.when(a > 0)
            def _():
                hop(out_ref.at[block], block, 1, down).start()

            hop(out_ref.at[block], block, 2, partner).start()

    for z in range(last + 1):
        hop(own_ref, z * 2 + 1 - b, 2, partner).wait_recv()
        hop(own_ref, z * 2 + b, 2, partner).wait_send()

        @pl.when((a < last) & (a >= z))
        def _():
            hop(own_ref, z * 2 + b, 0, partner).wait_send()

        @pl.when((a > 0) & (a <= z))
        def _():
            hop(own_ref, z * 2 + b, 1, partner).wait_send()

    mine.wait()


def gather(block, axis, n, collective_id):
    return pl.pallas_call(
        functools.partial(gather_kernel, axis, n),
        in_specs=[pl.BlockSpec(memory_space=pltpu.VMEM)],
        out_specs=pl.BlockSpec(memory_space=pl.ANY),
        out_shape=jax.ShapeDtypeStruct((n,) + block.shape, block.dtype),
        scratch_shapes=[
            pltpu.SemaphoreType.DMA,
            pltpu.SemaphoreType.DMA((n, 3)),
            pltpu.SemaphoreType.DMA((n,)),
        ],
        compiler_params=pltpu.CompilerParams(collective_id=collective_id, has_side_effects=True),
        name="gather",
    )(block)


def scatter_kernel(axis, n, compute, g_ref, out_ref, crossed, risen, fallen, going, send_sems, x_sems, up_sems, down_sems):
    me = lax.axis_index(axis)
    a, b = me // 2, me % 2
    last = n // 2 - 1
    up, down, partner = me + 2, me - 2, a * 2 + (1 - b)
    greet(axis, a, last, up, down, partner)
    rows = out_ref.shape[0]
    step = min(rows, 32)
    half = (last + 2) // 2
    high = a // half

    def place(t):
        return high * t + (1 - high) * (last - t)

    def cross(z):
        return pltpu.make_async_remote_copy(
            src_ref=g_ref.at[z * 2 + 1 - b], dst_ref=crossed.at[z], send_sem=send_sems.at[z, 0],
            recv_sem=x_sems.at[z], device_id={axis: partner}, device_id_type=pl.DeviceIdType.MESH,
        )

    def rise(z):
        return pltpu.make_async_remote_copy(
            src_ref=going.at[z], dst_ref=risen.at[z], send_sem=send_sems.at[z, 1],
            recv_sem=up_sems.at[z], device_id={axis: up}, device_id_type=pl.DeviceIdType.MESH,
        )

    def fall(z):
        return pltpu.make_async_remote_copy(
            src_ref=going.at[z], dst_ref=fallen.at[z], send_sem=send_sems.at[z, 2],
            recv_sem=down_sems.at[z], device_id={axis: down}, device_id_type=pl.DeviceIdType.MESH,
        )

    def add(target, parts):
        @pl.loop(0, rows // step)
        def _(i):
            at = pl.ds(pl.multiple_of(i * step, step), step)
            total = parts[0][at, :].astype(jnp.float32)
            for part in parts[1:]:
                total = total + part[at, :].astype(jnp.float32)
            target[at, :] = total.astype(target.dtype)

    if compute is None:
        for t in range(last + 1):
            cross(place(t)).start()
    else:
        @pl.loop(0, last + 1)
        def _(t):
            compute(place(t) * 2 + 1 - b)
            cross(place(t)).start()

        @pl.loop(0, last + 1)
        def _(t):
            compute(place(t) * 2 + b)

    for t in range(last + 1):
        z = place(t)
        cross(z).wait_recv()
        pair = [g_ref.at[z * 2 + b], crossed.at[z]]

        @pl.when(z > a)
        def _():
            @pl.when(a > 0)
            def _():
                rise(z).wait_recv()
                add(going.at[z], pair + [risen.at[z]])

            @pl.when(a == 0)
            def _():
                add(going.at[z], pair)

            rise(z).start()

        @pl.when(z < a)
        def _():
            @pl.when(a < last)
            def _():
                fall(z).wait_recv()
                add(going.at[z], pair + [fallen.at[z]])

            @pl.when(a == last)
            def _():
                add(going.at[z], pair)

            fall(z).start()

    pair = [g_ref.at[a * 2 + b], crossed.at[a]]

    @pl.when(a > 0)
    def _():
        rise(a).wait_recv()

    @pl.when(a < last)
    def _():
        fall(a).wait_recv()

    @pl.when(a == 0)
    def _():
        add(out_ref, pair + [fallen.at[a]])

    @pl.when(a == last)
    def _():
        add(out_ref, pair + [risen.at[a]])

    @pl.when((a > 0) & (a < last))
    def _():
        add(out_ref, pair + [risen.at[a], fallen.at[a]])

    for z in range(last + 1):
        cross(z).wait_send()

        @pl.when(z > a)
        def _():
            rise(z).wait_send()

        @pl.when(z < a)
        def _():
            fall(z).wait_send()


def scatter(parts, axis, collective_id):
    n, rows, columns = parts.shape
    half = n // 2
    blocks = pltpu.VMEM((half, rows, columns), parts.dtype)
    return pl.pallas_call(
        functools.partial(scatter_kernel, axis, n, None),
        in_specs=[pl.BlockSpec(memory_space=pltpu.VMEM)],
        out_specs=pl.BlockSpec(memory_space=pltpu.VMEM),
        out_shape=jax.ShapeDtypeStruct((rows, columns), jnp.bfloat16),
        scratch_shapes=[blocks] * 4
        + [
            pltpu.SemaphoreType.DMA((half, 3)),
            pltpu.SemaphoreType.DMA((half,)),
            pltpu.SemaphoreType.DMA((half,)),
            pltpu.SemaphoreType.DMA((half,)),
        ],
        compiler_params=pltpu.CompilerParams(
            collective_id=collective_id, has_side_effects=True, vmem_limit_bytes=40 << 20
        ),
        name="scatter",
    )(parts)


def attend_kernel(axis, n, bias_ref, q_ref, g_ref, kv_ref, out_ref, gq_ref, sum_ref, gkv_ref, *rest):
    def compute(block):
        attend_block(block, bias_ref, q_ref, g_ref, kv_ref, out_ref, gq_ref, gkv_ref)

    scatter_kernel(axis, n, compute, gkv_ref, sum_ref, *rest)


def attend(bias, queries, grad_out, kv, axis, collective_id):
    n, rows, columns = kv.shape
    half = n // 2
    blocks = pltpu.VMEM((half, rows, columns), jnp.bfloat16)
    vmem = pl.BlockSpec(memory_space=pltpu.VMEM)
    return pl.pallas_call(
        functools.partial(attend_kernel, axis, n),
        in_specs=[vmem] * 4,
        out_specs=[vmem] * 3,
        out_shape=[
            jax.ShapeDtypeStruct(queries.shape, jnp.bfloat16),
            jax.ShapeDtypeStruct(queries.shape, jnp.bfloat16),
            jax.ShapeDtypeStruct((rows, columns), jnp.bfloat16),
        ],
        scratch_shapes=[pltpu.VMEM(kv.shape, jnp.bfloat16)]
        + [blocks] * 4
        + [
            pltpu.SemaphoreType.DMA((half, 3)),
            pltpu.SemaphoreType.DMA((half,)),
            pltpu.SemaphoreType.DMA((half,)),
            pltpu.SemaphoreType.DMA((half,)),
        ],
        compiler_params=pltpu.CompilerParams(
            collective_id=collective_id, has_side_effects=True, vmem_limit_bytes=48 << 20
        ),
        name="attend",
    )(bias, queries, grad_out, kv)


def per_device(groups, text, src, lengths, kv_weight, queries, grad_out):
    dp, ctx = groups
    group = lax.axis_index("dp")
    samples = src.shape[0]
    share = ctx // dp
    tokens = text.shape[2]
    keys = 2 * tokens
    features = kv_weight.shape[0]
    columns = kv_weight.shape[2]
    hops = [
        (d * ctx + c, (c // share) * ctx + d * share + c % share)
        for d in range(dp)
        for c in range(ctx)
    ]
    mine = lax.ppermute(text[0], ("dp", "ctx"), hops)
    pieces = gather(mine.reshape(2 * tokens, -1), "ctx", ctx, 1)
    pieces = pieces.reshape(samples, share, 2, tokens, features // share)
    by_text = jnp.transpose(pieces, (0, 2, 3, 1, 4)).reshape(samples, 2, tokens, features)
    rows = jnp.stack(
        [lax.dynamic_index_in_dim(by_text, src[b], 0, keepdims=False) for b in range(samples)]
    )
    partial = jnp.einsum("betf,fec->betc", rows, kv_weight, preferred_element_type=jnp.float32)
    kv_local = scatter(partial.reshape(samples, keys, columns), "dp", 4)
    kv = gather(kv_local, "ctx", ctx, 2)
    own_lengths = lax.dynamic_index_in_dim(lengths, src[group], 0, keepdims=False)
    valid = jnp.arange(tokens, dtype=jnp.int32)[None, :] < own_lengths[:, None]
    bias = jnp.where(valid, 0.0, -1e30).astype(jnp.float32).reshape(1, keys)
    attended, grad_queries, grad_low = attend(bias, queries[0], grad_out[0], kv, "ctx", 3)
    grads = gather(grad_low, "dp", dp, 5)
    grads = grads.reshape(samples, 2, tokens, columns)
    grad_weight = jnp.einsum("betf,betc->fec", rows, grads, preferred_element_type=jnp.float32)
    return (attended[None], grad_queries[None], grad_weight)


def solution(mesh):
    placed = (
        P("dp", None, None, "ctx"),
        P(),
        P(),
        P("dp", None, "ctx"),
        P("dp", "ctx", None),
        P("dp", "ctx", None),
    )
    return jax.shard_map(
        functools.partial(per_device, (mesh.shape["dp"], mesh.shape["ctx"])),
        mesh=mesh,
        in_specs=placed,
        out_specs=(P("dp", "ctx", None), P("dp", "ctx", None), P("dp", None, "ctx")),
        check_vma=False,
    )
```

profile of v0, /device:TPU:0, one launch (start us, length us, event | category | flops | bytes accessed | tf_op | source)
XLA Modules:
  0.0 228.9 jit_solution(6128898298032050952)
XLA Ops:
  0.6 0.0 copy-start
  0.6 1.7 collective-permute-start
  2.3 1.5 fusion.3
  13.4 0.9 fusion.2
  14.3 0.1 compare_select_fusion
  14.4 0.0 collective-permute-done
  14.4 0.0 copy-start.12
  14.4 0.7 copy-done.12
  15.0 24.6 %gather.3 = bf16[8,256,256]{2,1,0:T(8,128)(2,1)} custom-call(bf16[256,256]{1,0:T(8,128)(2,1)} %bitcast.36), custom_call_target="tpu_custom_call" | custom-call | tf_op jit(solution)/shard_map/gather/pallas_call | solution.py:135
  39.6 3.3 %copy.9 = bf16[4,2,128,2,256]{4,3,2,0,1:T(2,128)(2,1)} copy(bf16[4,2,128,2,256]{4,2,1,3,0:T(8,128)(2,1)} %bitcast.32) | data formatting | bytes 2097152 | tf_op jit(solution)/shard_map/transpose | solution.py:345
  42.9 1.7 reshape.54
  44.6 0.1 constant_dynamic-slice_fusion.3
  44.7 0.0 copy-done
  44.7 0.0 copy-start.6
  44.7 0.0 copy-start.8
  44.7 0.0 copy-start.10
  44.7 0.7 copy-done.6
  45.4 0.1 copy-done.8
  45.5 0.1 copy-done.10
  45.6 1.4 convolution_bitcast_fusion.1
  47.0 0.3 copy.11
  47.3 29.7 %scatter.1.own_ref = bf16[256,1024]{1,0:T(8,128)(2,1)S(1)} custom-call(f32[4,256,1024]{2,1,0:T(8,128)S(1)} %bitcast.28), custom_call_target="tpu_custom_call" | custom-call | tf_op jit(solution)/shard_map/scatter/pallas_call | solution.py:273
  77.0 0.0 copy-start.1
  77.1 0.8 copy-done.1
  77.8 49.4 %gather.4.kv_ref = bf16[8,256,1024]{2,1,0:T(8,128)(2,1)} custom-call(bf16[256,1024]{1,0:T(8,128)(2,1)} %copy-done.1), custom_call_target="tpu_custom_call" | custom-call | tf_op jit(solution)/shard_map/gather/pallas_call | solution.py:135
  127.2 62.5 %attend.1 = (bf16[256,4096]{1,0:T(8,128)(2,1)S(1)}, bf16[256,4096]{1,0:T(8,128)(2,1)S(1)}, bf16[256,1024]{1,0:T(8,128)(2,1)S(1)}) custom-call(f32[1,256]{1,0:T(1,128)S(1)} %bitcast.31, bf16[256,4096]{1,0:T(8,128)(2,1)} %bitcast.33, bf16[256,4096]{1,0:T(8,128)(2,1)} %bitcast.34, bf16[8,256,1024]{2,1,0:T(8,128)(2,1)} %gather.4.kv_ref), custom_call_target="tpu_custom_call" | custom-call | tf_op jit(solution)/shard_map/attend/pallas_call | solution.py:304
  189.7 0.0 copy-start.2
  189.8 1.3 copy-done.2
  191.1 0.0 copy-start.4
  191.1 1.3 copy-done.4
  192.4 0.0 copy-start.5
  192.4 0.8 copy-done.5
  193.2 0.0 copy-start.7
  193.2 0.0 copy-start.9
  193.2 0.0 copy-start.11
  193.2 19.0 %gather.5 = bf16[4,256,1024]{2,1,0:T(8,128)(2,1)} custom-call(bf16[256,1024]{1,0:T(8,128)(2,1)} %copy-done.5), custom_call_target="tpu_custom_call" | custom-call | tf_op jit(solution)/shard_map/gather/pallas_call | solution.py:135
  212.2 0.0 copy-done.7
  212.2 0.0 copy-done.9
  212.2 0.0 copy-done.11
  212.2 4.8 %convolution_bitcast_fusion = f32[512,2,1024]{0,2,1:T(8,128)} fusion(bf16[4,2,128,1024]{3,2,1,0:T(8,128)(2,1)} %bitcast.35, bf16[1,2,128,512]{3,2,0,1:T(8,128)(2,1)S(1)} %copy-done.7, bf16[1,2,128,512]{3,2,0,1:T(8,128)(2,1)S(1)} %copy-done.9, bf16[1,2,128,512]{3,2,0,1:T(8,128)(2,1)S(1)} %copy-done.11, bf16[1,2,128,512]{3,2,0,1:T(8,128)(2,1)S(1)} %get-tuple-element.12), kind=kOutput, calls=%fused_computation | convolution fusion | flops 1075314688 | bytes 7340032 | tf_op jit(solution)/shard_map/betf,betc->fec/dot_general | solution.py:358
  217.0 7.3 %copy.13 = f32[512,2,1024]{2,1,0:T(2,128)} copy(f32[512,2,1024]{0,2,1:T(8,128)} %convolution_bitcast_fusion) | data formatting | bytes 8388608
  224.3 0.0 copy-start.3
  224.3 3.3 %copy.25 = bf16[1,256,4096]{2,1,0:T(8,128)(2,1)} copy(bf16[1,256,4096]{2,1,0:T(8,128)(2,1)} %bitcast.30) | data formatting | bytes 4194304
  227.6 0.0 copy-done.3
  227.6 1.3 copy.26
Async XLA Ops:
  0.6 44.1 %copy-start = (bf16[512,2,1024]{2,1,0:T(2,128)(2,1)S(1)}, bf16[512,2,1024]{2,1,0:T(2,128)(2,1)}, u32[]{:S(2)}) copy-start(bf16[512,2,1024]{2,1,0:T(2,128)(2,1)} %param.9) | copy-start | bytes 6291460
  0.6 13.7 %collective-permute-start = (bf16[2,128,256]{2,1,0:T(8,128)(2,1)}, bf16[2,128,256]{2,1,0:T(8,128)(2,1)S(1)}, u32[]{:S(2)}, u32[]{:S(2)}) collective-permute-start(bf16[2,128,256]{2,1,0:T(8,128)(2,1)} %bitcast.37), channel_id=1, source_target_pairs={{0,0},{1,1},{2,8},{3,9},{4,16},{5,17},{6,24},{7,25},{8,2},{9,3},{1... | collective-permute-start | bytes 393224 | tf_op jit(solution)/shard_map/ppermute | solution.py:342
  14.4 0.7 copy-start.12
  44.7 0.7 copy-start.6
  44.7 0.8 copy-start.8
  44.7 0.9 copy-start.10
  77.0 0.8 copy-start.1
  189.7 1.3 copy-start.2
  191.1 1.3 copy-start.4
  192.4 0.8 copy-start.5
  193.2 19.0 %copy-start.7 = (bf16[1,2,128,512]{3,2,0,1:T(8,128)(2,1)S(1)}, bf16[1,2,128,512]{3,2,0,1:T(8,128)(2,1)}, u32[]{:S(2)}) copy-start(bf16[1,2,128,512]{3,2,0,1:T(8,128)(2,1)} %copy-done.6) | copy-start | bytes 786436
  193.2 19.0 %copy-start.9 = (bf16[1,2,128,512]{3,2,0,1:T(8,128)(2,1)S(1)}, bf16[1,2,128,512]{3,2,0,1:T(8,128)(2,1)}, u32[]{:S(2)}) copy-start(bf16[1,2,128,512]{3,2,0,1:T(8,128)(2,1)} %copy-done.8) | copy-start | bytes 786436
  193.2 19.0 %copy-start.11 = (bf16[1,2,128,512]{3,2,0,1:T(8,128)(2,1)S(1)}, bf16[1,2,128,512]{3,2,0,1:T(8,128)(2,1)}, u32[]{:S(2)}) copy-start(bf16[1,2,128,512]{3,2,0,1:T(8,128)(2,1)} %copy-done.10) | copy-start | bytes 786436
  224.3 3.3 %copy-start.3 = (bf16[256,4096]{1,0:T(8,128)(2,1)S(1)}, bf16[256,4096]{1,0:T(8,128)(2,1)}, u32[]{:S(2)}) copy-start(bf16[256,4096]{1,0:T(8,128)(2,1)} %copy-done.2) | copy-start | bytes 6291460
where the time goes:
time: 230 us; the launch traced here: 229 us
  Pallas kernels  185 us (80%)
  local copies, waits for them, and re-layouts  25.4 us (11%)
  between operations  10.4 us (5%)
  matrix products  6.24 us (3%)
    pallas_call x3, Pallas kernels, gather(): pl.pallas_call(functools.partial(gather_kernel, axis, n), in_specs=[pl.Bl...  92.9 us
    pallas_call x1, Pallas kernels, attend(): pl.pallas_call(functools.partial(attend_kernel, axis, n), in_specs=[vmem]...  62.5 us
    pallas_call x1, Pallas kernels, scatter(): pl.pallas_call(functools.partial(scatter_kernel, axis, n, None), in_specs...  29.7 us
    unnamed x29, local copies, waits for them, and re-layouts  17.7 us
    dot_general x1, matrix products, per_device(): jnp.einsum('betf,betc->fec', rows, grads, preferred_element_type=jnp.floa...  4.85 us
  transfers between devices with their start and end apart: 1, of which 0 were waited for; matrix products, arithmetic and copies ran while one was open for 1% of the time, Pallas kernels for 0%

commit v1 on v0

v1 whole, which is shorter than its diff:
```python
import functools
import math

import jax
import jax.numpy as jnp
from jax import lax
from jax.experimental import pallas as pl
from jax.experimental.pallas import tpu as pltpu
from jax.sharding import PartitionSpec as P

HEAD = 128
PAIR = 2 * HEAD
STEP = 32
MESH = pl.DeviceIdType.MESH
VMEM = pl.BlockSpec(memory_space=pltpu.VMEM)
SMEM = pl.BlockSpec(memory_space=pltpu.SMEM)
ANY = pl.BlockSpec(memory_space=pl.ANY)
DMA = pltpu.SemaphoreType.DMA


def dot(a, b, dims):
    return lax.dot_general(a, b, (dims, ((), ())), preferred_element_type=jnp.float32)


def remote(src, dst, send_sem, recv_sem, target):
    return pltpu.make_async_remote_copy(
        src_ref=src, dst_ref=dst, send_sem=send_sem, recv_sem=recv_sem, device_id=target, device_id_type=MESH
    )


class Place:
    def __init__(self, dp, ctx):
        self.rows, self.planes = dp // 2, ctx // 2
        self.last = self.planes - 1
        self.d, self.c = lax.axis_index("dp"), lax.axis_index("ctx")
        self.row, self.core = self.d // 2, self.d % 2
        self.a, self.b = self.c // 2, self.c % 2
        self.up = {"ctx": self.c + 2}
        self.down = {"ctx": self.c - 2}
        self.side = {"ctx": self.a * 2 + 1 - self.b}
        self.twin = {"dp": self.row * 2 + 1 - self.core}

    def at_row(self, row):
        return {"dp": row * 2 + self.core}

    def greet(self):
        barrier = pltpu.get_barrier_semaphore()

        def hello(target):
            pl.semaphore_signal(barrier, inc=1, device_id=target, device_id_type=MESH)

        hello(self.side)
        hello(self.twin)
        for j in range(self.rows):

            @pl.when(self.row != j)
            def _():
                hello(self.at_row(j))

        @pl.when(self.a < self.last)
        def _():
            hello(self.up)

        @pl.when(self.a > 0)
        def _():
            hello(self.down)

        fixed = 1 + self.rows
        if self.last == 0:
            pl.semaphore_wait(barrier, fixed)
        else:

            @pl.when((self.a > 0) & (self.a < self.last))
            def _():
                pl.semaphore_wait(barrier, fixed + 2)

            @pl.when((self.a == 0) | (self.a == self.last))
            def _():
                pl.semaphore_wait(barrier, fixed + 1)


def text_kernel(dp, ctx, src_ref, own_ref, weight_ref, chosen_ref, rows_ref, other_ref, text,
                own_sem, w_sems, row_send, row_recv, line_send, line_recv, twin_send, twin_recv):
    me = Place(dp, ctx)
    rows, a, b, last = me.rows, me.a, me.b, me.last
    share = ctx // dp
    width = own_ref.shape[2]
    features = share * width
    me.greet()
    weights = remote(weight_ref, other_ref, w_sems.at[0], w_sems.at[1], me.twin)

    def spot(piece, core):
        return pl.ds(pl.multiple_of((piece + core * share) % (2 * share) * width, width), width)

    def block(sample, piece, core):
        return text.at[:, sample, :, spot(piece, core)]

    home = me.c // (2 * share)
    piece = me.c % (2 * share)
    mine = pltpu.make_async_copy(own_ref, block(me.d, piece, me.core), own_sem)

    def to_row(row, sample_row):
        return remote(own_ref, block(sample_row * 2 + me.core, piece, me.core), row_send,
                      row_recv.at[sample_row], me.at_row(row))

    def line(i, side, j, way, target):
        p = i * 2 + side
        where = block(j * 2 + me.core, p, me.core)
        return remote(where, where, line_send.at[p, j, way], line_recv.at[p, j], target)

    def across(p, j):
        return remote(block(j * 2 + me.core, p, me.core), block(j * 2 + me.core, p, 1 - me.core),
                      twin_send.at[p, j], twin_recv.at[p, j], me.twin)

    for row in range(rows):

        @pl.when((home == row) & (me.row != row))
        def _():
            to_row(row, me.row).start()

        @pl.when((home == row) & (me.row == row))
        def _():
            mine.start()

    weights.start()
    first = me.row * share
    high = jnp.where(2 * a >= 2 * first + share, 1, 0)
    for t in range(share):
        i = high * (share - 1 - t) + (1 - high) * t
        plane = first + i
        for j_at in range(rows):
            j = (me.row + j_at) % rows

            @pl.when(a == plane)
            def _():
                if j_at == 0:
                    mine.wait()
                else:
                    to_row(0, j).wait_recv()

            @pl.when(a > plane)
            def _():
                line(i, b, j, 0, me.up).wait_recv()

            @pl.when(a < plane)
            def _():
                line(i, b, j, 1, me.down).wait_recv()

            @pl.when((a >= plane) & (a < last))
            def _():
                line(i, b, j, 0, me.up).start()

            @pl.when((a <= plane) & (a > 0))
            def _():
                line(i, b, j, 1, me.down).start()

            line(i, b, j, 2, me.side).start()
            across(i * 2 + b, j).start()

    for t in range(share):
        i = high * (share - 1 - t) + (1 - high) * t
        for j_at in range(rows):
            j = (me.row + j_at) % rows
            line(i, 1 - b, j, 2, me.side).wait_recv()
            across(i * 2 + 1 - b, j).start()

    for p in range(2 * share):
        for j in range(rows):
            across(p, j).wait_recv()
    for b_at in range(dp):
        for e in range(2):
            rows_ref[e, b_at] = text[e, src_ref[b_at], :, pl.ds(0, features)]
    for j in range(rows):
        for e in range(2):
            chosen_ref[e, j] = text[e, src_ref[j * 2 + me.core]]
    for row in range(rows):

        @pl.when((home == row) & (me.row != row))
        def _():
            to_row(row, me.row).wait_send()

    for p in range(2 * share):
        for j in range(rows):
            across(p, j).wait_send()
    for i in range(share):
        plane = first + i
        for j in range(rows):

            @pl.when((a >= plane) & (a < last))
            def _():
                line(i, b, j, 0, me.up).wait_send()

            @pl.when((a <= plane) & (a > 0))
            def _():
                line(i, b, j, 1, me.down).wait_send()

            line(i, b, j, 2, me.side).wait_send()
    weights.wait()


def gather_text(src, own, weight, dp, ctx):
    tokens, width = own.shape[1:]
    share = ctx // dp
    rows = dp // 2
    kind = own.dtype
    pieces = 2 * share
    return pl.pallas_call(
        functools.partial(text_kernel, dp, ctx),
        in_specs=[SMEM, VMEM, ANY],
        out_specs=[VMEM, VMEM, ANY],
        out_shape=[
            jax.ShapeDtypeStruct((2, rows, tokens, pieces * width), kind),
            jax.ShapeDtypeStruct((2, dp, tokens, share * width), kind),
            jax.ShapeDtypeStruct(weight.shape, weight.dtype),
        ],
        scratch_shapes=[
            pltpu.VMEM((2, dp, tokens, pieces * width), kind),
            DMA,
            DMA((2,)),
            DMA,
            DMA((rows,)),
            DMA((pieces, rows, 3)),
            DMA((pieces, rows)),
            DMA((pieces, rows)),
            DMA((pieces, rows)),
        ],
        compiler_params=pltpu.CompilerParams(collective_id=1, has_side_effects=True, vmem_limit_bytes=16 << 20),
        name="gather_text",
    )(src, own, weight)


def sublayer_kernel(dp, ctx, cut, src_ref, lengths_ref, part_ref, q_any, g_any, out_ref, gq_ref, grads_ref,
                    q_ref, g_ref, sums, kv, gkv, crossed0, risen0, fallen0, going0,
                    risen1, fallen1, going1, crossed1,
                    in_sems, y_send, y_recv, ag_send, ag_recv, x0_send, x0_recv,
                    up0_send, up0_recv, down0_send, down0_recv,
                    up1_send, up1_recv, down1_send, down1_recv, x1_send, x1_recv,
                    dp_send, dp_recv, twin_send):
    me = Place(dp, ctx)
    nrows, a, b, last = me.rows, me.a, me.b, me.last
    planes = me.planes
    rounds = kv.shape[0]
    keys = kv.shape[2]
    tokens = keys // 2
    own = me.c
    load_q = pltpu.make_async_copy(q_any, q_ref, in_sems.at[0])
    load_g = pltpu.make_async_copy(g_any, g_ref, in_sems.at[1])
    load_q.start()
    load_g.start()
    me.greet()
    parts = (pl.ds(0, cut), pl.ds(cut, keys - cut))

    def columns(r):
        return pl.ds(pl.multiple_of(r * PAIR, PAIR), PAIR)

    def partial(r, row, sender):
        return remote(part_ref.at[:, row, :, columns(r)], sums.at[r, sender], y_send.at[r, row],
                      y_recv.at[r, sender], me.at_row(row))

    def ag(r, part, block, way, target):
        where = kv.at[r, block, parts[part], :]
        return remote(where, where, ag_send.at[r, part, block, way], ag_recv.at[r, part, block], target)

    def ag_wait(r, part, block):
        ag(r, part, block, 2, me.side).wait_recv()

    def send_up(r, part, block):
        @pl.when(a < last)
        def _():
            ag(r, part, block, 0, me.up).start()

    def send_down(r, part, block):
        @pl.when(a > 0)
        def _():
            ag(r, part, block, 1, me.down).start()

    def start_round(r):
        for j in range(nrows):

            @pl.when(me.row != j)
            def _():
                partial(r, j, j).wait_recv()

        for e in range(2):
            total = part_ref[e, me.row, :, columns(r)]
            for j_at in range(1, nrows):
                total = total + sums[r, (me.row + j_at) % nrows, e]
            kv[r, own, e * tokens:(e + 1) * tokens, :] = total.astype(kv.dtype)
        ag(r, 1, own, 2, me.side).start()
        send_up(r, 0, own)
        send_down(r, 0, own)
        ag(r, 0, own, 2, me.side).start()
        send_up(r, 1, own)
        send_down(r, 1, own)

    def relay_side(r):
        block = a * 2 + 1 - b
        ag_wait(r, 1, block)
        send_up(r, 1, block)
        send_down(r, 1, block)

    def relay(r, s):
        @pl.when(a >= s)
        def _():
            base = (a - s) * 2
            ag_wait(r, 0, base + b)
            send_up(r, 0, base + b)
            ag(r, 0, base + b, 2, me.side).start()
            for side in range(2):
                ag_wait(r, 1, base + side)
                send_up(r, 1, base + side)

        @pl.when(a + s <= last)
        def _():
            base = (a + s) * 2
            ag_wait(r, 0, base + b)
            send_down(r, 0, base + b)
            ag(r, 0, base + b, 2, me.side).start()
            for side in range(2):
                ag_wait(r, 1, base + side)
                send_down(r, 1, base + side)

    scale = 1.0 / math.sqrt(HEAD)
    position = lax.broadcasted_iota(jnp.int32, (1, keys), 1)
    text_at = src_ref[me.d]
    bound = jnp.where(position < tokens, lengths_ref[text_at, 0], lengths_ref[text_at, 1] + tokens)
    bias = jnp.where(position < bound, 0.0, -1e30).astype(jnp.float32)

    def attend(r, block):
        at = pl.ds(pl.multiple_of((block * rounds + r) * HEAD, HEAD), HEAD)
        q = q_ref[:, at]
        g = g_ref[:, at]
        key = kv[r, block, :, :HEAD]
        value = kv[r, block, :, HEAD:]
        scores = dot(q, key, ((1,), (1,))) * scale + bias
        top = jnp.max(scores, axis=-1, keepdims=True)
        weights = jnp.exp(scores - top)
        probs = weights * (1.0 / jnp.sum(weights, axis=-1, keepdims=True))
        probs_low = probs.astype(jnp.bfloat16)
        out_ref[:, at] = dot(probs_low, value, ((1,), (0,))).astype(jnp.bfloat16)
        grad_probs = dot(g, value, ((1,), (1,)))
        delta = jnp.sum(probs * grad_probs, axis=-1, keepdims=True)
        grad_scores = (probs * (grad_probs - delta) * scale).astype(jnp.bfloat16)
        gq_ref[:, at] = dot(grad_scores, key, ((1,), (0,))).astype(jnp.bfloat16)
        gkv[r, block, :, :HEAD] = dot(grad_scores, q, ((0,), (0,))).astype(gkv.dtype)
        gkv[r, block, :, HEAD:] = dot(probs_low, g, ((0,), (0,))).astype(gkv.dtype)

    def cross0(r, z):
        return remote(gkv.at[r, z * 2 + 1 - b, parts[0], :], crossed0.at[r, z], x0_send.at[r, z],
                      x0_recv.at[r, z], me.side)

    def work(r, s):
        @pl.loop(0, 4)
        def _(t):
            way, foreign = t // 2, t % 2
            far = s - foreign
            z = a + far * (2 * way - 1)
            block = z * 2 + b + foreign * (1 - 2 * b)

            @pl.when((z >= 0) & (z <= last) & (far >= 0) & (far <= last) & ((far > 0) | (way == 0)))
            def _():
                @pl.when(foreign == 1)
                def _():
                    ag_wait(r, 0, block)

                attend(r, block)

                @pl.when(foreign == 1)
                def _():
                    cross0(r, z).start()

    def chain0(r, z, rising):
        if rising:
            return remote(going0.at[r, z], risen0.at[r, z], up0_send.at[r, z], up0_recv.at[r, z], me.up)
        return remote(going0.at[r, z], fallen0.at[r, z], down0_send.at[r, z], down0_recv.at[r, z], me.down)

    def chain1(r, z, side, rising, source):
        if rising:
            return remote(source, risen1.at[r, z, side], up1_send.at[r, z, side], up1_recv.at[r, z, side], me.up)
        return remote(source, fallen1.at[r, z, side], down1_send.at[r, z, side], down1_recv.at[r, z, side], me.down)

    def add(target, terms):
        @pl.loop(0, target.shape[0] // STEP)
        def _(i):
            at = pl.ds(pl.multiple_of(i * STEP, STEP), STEP)
            total = terms[0][at, :].astype(jnp.float32)
            for term in terms[1:]:
                total = total + term[at, :].astype(jnp.float32)
            target[at, :] = total.astype(target.dtype)

    def pass_on(r, z, rising, begins):
        arrived0 = risen0 if rising else fallen0
        arrived1 = risen1 if rising else fallen1
        for side in range(2):
            source = gkv.at[r, z * 2 + side, parts[1], :]
            if not begins:
                target = going1.at[r, z, side]
                chain1(r, z, side, rising, target).wait_recv()
                add(target, [source, arrived1.at[r, z, side]])
                source = target
            chain1(r, z, side, rising, source).start()
        cross0(r, z).wait_recv()
        terms = [gkv.at[r, z * 2 + b, parts[0], :], crossed0.at[r, z]]
        if not begins:
            chain0(r, z, rising).wait_recv()
            terms.append(arrived0.at[r, z])
        add(going0.at[r, z], terms)
        chain0(r, z, rising).start()

    def reduce_step(r, s):
        @pl.when(a == s)
        def _():
            for z in range(last, s, -1):
                pass_on(r, z, True, s == 0)

        @pl.when(a == last - s)
        def _():
            for z in range(0, last - s):
                pass_on(r, z, False, s == 0)

    def own_terms(r, low, high, side=None):
        terms = []
        if side is None:
            terms += [risen0.at[r, a]] * low + [fallen0.at[r, a]] * high
        else:
            terms += [risen1.at[r, a, side]] * low + [fallen1.at[r, a, side]] * high
        return terms

    def cross1(r):
        return remote(going1.at[r, a, 1 - b], crossed1.at[r], x1_send.at[r], x1_recv.at[r], me.side)

    def by_place(body):
        @pl.when(a == 0)
        def _():
            body(0, 1)

        @pl.when(a == last)
        def _():
            body(1, 0)

        @pl.when((a > 0) & (a < last))
        def _():
            body(1, 1)

    def finish(r):
        def body(low, high):
            for rising in (True,) * low + (False,) * high:
                for side in range(2):
                    chain1(r, a, side, rising, going1.at[r, a, side]).wait_recv()
            add(going1.at[r, a, 1 - b],
                [gkv.at[r, a * 2 + 1 - b, parts[1], :]] + own_terms(r, low, high, 1 - b))
            cross1(r).start()
            for rising in (True,) * low + (False,) * high:
                chain0(r, a, rising).wait_recv()
            cross0(r, a).wait_recv()
            add(grads_ref.at[me.d, parts[0], columns(r)],
                [gkv.at[r, own, parts[0], :], crossed0.at[r, a]] + own_terms(r, low, high))

        by_place(body)

    def share_grads(r, d, way, target):
        where = grads_ref.at[d, :, columns(r)]
        return remote(where, where, dp_send.at[r, way], dp_recv.at[r, d], target)

    def hand_over(r, d):
        where = grads_ref.at[d, :, columns(r)]
        return remote(where, where, twin_send.at[r, d // 2], dp_recv.at[r, d], me.twin)

    def close(r):
        cross1(r).wait_recv()

        def body(low, high):
            add(grads_ref.at[me.d, parts[1], columns(r)],
                [gkv.at[r, own, parts[1], :], crossed1.at[r]] + own_terms(r, low, high, b))

        by_place(body)
        for j in range(nrows):

            @pl.when(me.row != j)
            def _():
                share_grads(r, me.d, j, me.at_row(j)).start()

        hand_over(r, me.d).start()

    def spread(r):
        for j in range(nrows):

            @pl.when(me.row != j)
            def _():
                d = j * 2 + me.core
                share_grads(r, d, j, me.at_row(j)).wait_recv()
                hand_over(r, d).start()

    @pl.loop(0, rounds)
    def _(r):
        for j in range(nrows):

            @pl.when(me.row != j)
            def _():
                partial(r, j, me.row).start()

    start_round(0)
    load_q.wait()
    load_g.wait()

    @pl.loop(0, rounds + 1)
    def _(i):
        for s in range(planes):

            @pl.when(i > 0)
            def _():
                reduce_step(i - 1, s)

            @pl.when(i < rounds)
            def _():
                if s == 0:
                    relay_side(i)
                else:
                    relay(i, s)
                if s == last:

                    @pl.when(i + 1 < rounds)
                    def _():
                        start_round(i + 1)

                work(i, s)

        @pl.when(i > 1)
        def _():
            close(i - 2)

        @pl.when(i > 0)
        def _():
            finish(i - 1)

        @pl.when(i < rounds)
        def _():
            work(i, planes)

        @pl.when(i > 2)
        def _():
            spread(i - 3)

    close(rounds - 1)
    for r in range(max(rounds - 2, 0), rounds):
        spread(r)

    @pl.loop(0, rounds)
    def _(r):
        for j in range(nrows):
            hand_over(r, j * 2 + 1 - me.core).wait_recv()
            hand_over(r, j * 2 + me.core).wait_send()

            @pl.when(me.row != j)
            def _():
                partial(r, j, me.row).wait_send()
                share_grads(r, me.d, j, me.at_row(j)).wait_send()

        ag(r, 1, own, 2, me.side).wait_send()
        cross1(r).wait_send()
        for z in range(planes):
            cross0(r, z).wait_send()
            ag(r, 0, z * 2 + b, 2, me.side).wait_send()

            @pl.when((a < last) & (z <= a))
            def _():
                ag(r, 0, z * 2 + b, 0, me.up).wait_send()
                for side in range(2):
                    ag(r, 1, z * 2 + side, 0, me.up).wait_send()

            @pl.when((a > 0) & (z >= a))
            def _():
                ag(r, 0, z * 2 + b, 1, me.down).wait_send()
                for side in range(2):
                    ag(r, 1, z * 2 + side, 1, me.down).wait_send()

            for rising in (True, False):

                @pl.when((z > a) if rising else (z < a))
                def _():
                    chain0(r, z, rising).wait_send()
                    for side in range(2):
                        chain1(r, z, side, rising, going1.at[r, z, side]).wait_send()


def sublayer(src, lengths, part, queries, grad_out, dp, ctx):
    _, rows, tokens, columns = part.shape
    rounds = columns // PAIR
    keys = 2 * tokens
    planes = ctx // 2
    cut = keys * 5 // 8 // STEP * STEP
    low = jnp.bfloat16
    first = pltpu.VMEM((rounds, planes, cut, PAIR), low)
    second = pltpu.VMEM((rounds, planes, 2, keys - cut, PAIR), low)
    whole = pltpu.VMEM((rounds, ctx, keys, PAIR), low)
    return pl.pallas_call(
        functools.partial(sublayer_kernel, dp, ctx, cut),
        in_specs=[SMEM, SMEM, VMEM, ANY, ANY],
        out_specs=[VMEM, VMEM, VMEM],
        out_shape=[
            jax.ShapeDtypeStruct(queries.shape, low),
            jax.ShapeDtypeStruct(queries.shape, low),
            jax.ShapeDtypeStruct((dp, keys, columns), low),
        ],
        scratch_shapes=[
            pltpu.VMEM(queries.shape, low),
            pltpu.VMEM(queries.shape, low),
            pltpu.VMEM((rounds, rows, 2, tokens, PAIR), jnp.float32),
            whole,
            whole,
            first,
            first,
            first,
            first,
            second,
            second,
            second,
            pltpu.VMEM((rounds, keys - cut, PAIR), low),
            DMA((2,)),
            DMA((rounds, rows)),
            DMA((rounds, rows)),
            DMA((rounds, 2, ctx, 3)),
            DMA((rounds, 2, ctx)),
        ]
        + [DMA((rounds, planes))] * 6
        + [DMA((rounds, planes, 2))] * 4
        + [
            DMA((rounds,)),
            DMA((rounds,)),
            DMA((rounds, rows)),
            DMA((rounds, dp)),
            DMA((rounds, rows)),
        ],
        compiler_params=pltpu.CompilerParams(collective_id=2, has_side_effects=True, vmem_limit_bytes=50 << 20),
        name="sublayer",
    )(src, lengths, part, queries, grad_out)


def weight_kernel(rows_ref, grads_ref, att_ref, gq_ref, out_ref, att_out, gq_out, buffer, sems):
    keep_att = pltpu.make_async_copy(att_ref, att_out, sems.at[0])
    keep_gq = pltpu.make_async_copy(gq_ref, gq_out, sems.at[1])
    keep_att.start()
    keep_gq.start()
    dp, keys, columns = grads_ref.shape
    tokens = keys // 2
    features = rows_ref.shape[3]
    lanes = columns // HEAD
    stride = 2 * lanes
    size = HEAD

    def ship(i):
        at = pl.ds(i * size * stride, size * stride)
        return pltpu.make_async_copy(buffer.at[at, :], out_ref.at[at, :], sems.at[2 + i])

    for i in range(features // size):
        for e in range(2):
            left = rows_ref[e, :, :, i * size:(i + 1) * size].reshape(dp * tokens, size)
            for j in range(columns // PAIR):
                right = grads_ref[:, e * tokens:(e + 1) * tokens, j * PAIR:(j + 1) * PAIR].reshape(dp * tokens, PAIR)
                block = dot(left, right, ((0,), (0,)))
                for half in range(2):
                    buffer[pl.ds(i * size * stride + (2 * j + half) * 2 + e, size, stride), :] = (
                        block[:, half * HEAD:(half + 1) * HEAD]
                    )
        ship(i).start()
    for i in range(features // size):
        ship(i).wait()
    keep_att.wait()
    keep_gq.wait()


def finish_weight(rows, grads, attended, grad_queries):
    dp, keys, columns = grads.shape
    features = rows.shape[3]
    lanes = columns // HEAD
    flat = (features * lanes * 2, HEAD)
    weight, attended, grad_queries = pl.pallas_call(
        weight_kernel,
        in_specs=[VMEM, VMEM, VMEM, VMEM],
        out_specs=[ANY, ANY, ANY],
        out_shape=[
            jax.ShapeDtypeStruct(flat, jnp.float32),
            jax.ShapeDtypeStruct(attended.shape, attended.dtype),
            jax.ShapeDtypeStruct(attended.shape, attended.dtype),
        ],
        scratch_shapes=[pltpu.VMEM(flat, jnp.float32), DMA((2 + features // HEAD,))],
        compiler_params=pltpu.CompilerParams(vmem_limit_bytes=24 << 20),
        name="finish_weight",
    )(rows, grads, attended, grad_queries)
    weight = weight.reshape(features, lanes, 2, HEAD).transpose(0, 2, 1, 3).reshape(features, 2, columns)
    return attended, grad_queries, weight


def per_device(dp, ctx, text, src, lengths, kv_weight, queries, grad_out):
    features = kv_weight.shape[0]
    chosen, rows, other = gather_text(src, text[0], kv_weight, dp, ctx)
    dims = "ejtf,fec->ejtc"
    part = jnp.einsum(dims, chosen[..., :features], kv_weight, preferred_element_type=jnp.float32)
    part = part + jnp.einsum(dims, chosen[..., features:], other, preferred_element_type=jnp.float32)
    attended, grad_queries, grads = sublayer(src, lengths, part, queries[0], grad_out[0], dp, ctx)
    attended, grad_queries, weight = finish_weight(rows, grads, attended, grad_queries)
    return (attended[None], grad_queries[None], weight)


def solution(mesh):
    placed = (
        P("dp", None, None, "ctx"),
        P(),
        P(),
        P("dp", None, "ctx"),
        P("dp", "ctx", None),
        P("dp", "ctx", None),
    )
    return jax.shard_map(
        functools.partial(per_device, mesh.shape["dp"], mesh.shape["ctx"]),
        mesh=mesh,
        in_specs=placed,
        out_specs=(P("dp", "ctx", None), P("dp", "ctx", None), P("dp", None, "ctx")),
        check_vma=False,
    )
```

time: 230 us -> 188 us (0.82)
  local copies, waits for them, and re-layouts: 25.4 us -> 7.78 us
  between operations: 10.4 us -> 0.68 us
  Pallas kernels: 185 us -> 176 us
  matrix products: 6.24 us -> 3.21 us
    unnamed x29 -> x15, local copies, waits for them, and re-layouts: 17.7 us -> 7.78 us
    pallas_call x5 -> x3, Pallas kernels: 185 us -> 176 us  [the longest x1 153 us: sublayer(): pl.pallas_call(functools.partial(sublayer_kernel, dp, ctx, cut), in_specs...]
    transpose x2 -> x0, local copies, waits for them, and re-layouts: 3.58 us -> none  [the longest x1 3.27 us: per_device(): jnp.transpose(pieces, (0, 2, 3, 1, 4)).reshape(samples, 2, tokens, features)]
    dot_general x2, matrix products: 6.24 us -> 3.21 us  [the longest x1 2.31 us: per_device(): jnp.einsum(dims, chosen[..., :features], kv_weight, preferred_element_typ...]
  transfers between devices with their start and end apart: 1 -> 0, of which waited for: 0 -> 0; matrix products, arithmetic and copies ran while one was open for 1% -> 0% of each run, Pallas kernels for 0% -> 0%
where the time goes in v1:
time: 188 us
  Pallas kernels  176 us (94%)
  local copies, waits for them, and re-layouts  7.78 us (4%)
  matrix products  3.21 us (2%)
    pallas_call x1, Pallas kernels, sublayer(): pl.pallas_call(functools.partial(sublayer_kernel, dp, ctx, cut), in_specs...  153 us
    pallas_call x1, Pallas kernels, gather_text(): pl.pallas_call(functools.partial(text_kernel, dp, ctx), in_specs=[SMEM, V...  19.6 us
    unnamed x15, local copies, waits for them, and re-layouts  7.78 us

profile of v1, /device:TPU:0, one launch (start us, length us, event | category | flops | bytes accessed | tf_op | source)
XLA Modules:
  0.0 187.5 jit_solution(12068796517313350524)
XLA Ops:
  0.6 0.8 copy.11.lengths_ref
  1.4 0.0 copy-start
  1.4 1.6 copy-done
  3.0 0.0 copy-start.4
  3.0 0.9 copy-done.4
  3.9 0.0 copy-start.5
  3.9 0.7 copy-done.5
  4.5 19.6 %gather_text.1 = (bf16[2,2,128,1024]{3,2,1,0:T(8,128)(2,1)S(1)}, bf16[2,4,128,512]{3,2,1,0:T(8,128)(2,1)S(1)}, bf16[512,2,1024]{2,1,0:T(2,128)(2,1)S(1)}) custom-call(s32[4]{0:T(128)S(1)} %copy-done.5, bf16[2,128,256]{2,1,0:T(8,128)(2,1)S(1)} %bitcast.14, bf16[512,2,1024]{2,1,0:T(2,128)(2,1)S(1)} %copy-done), custom_call_target="tpu_custom_call" | custom-call | tf_op jit(solution)/shard_map/gather_text/pallas_call | solution.py:207
  24.2 0.0 copy-start.1
  24.2 0.9 fusion
  25.1 0.7 copy-done.1
  25.8 0.0 copy-start.6
  25.8 2.3 %fusion.4.part_ref = f32[2,2,128,1024]{3,2,1,0:T(8,128)} fusion(f32[2,2,128,1024]{3,2,1,0:T(8,128)S(1)} %fusion, bf16[512,2,1024,1]{2,1,0,3:T(2,128)(2,1)S(1)} %bitcast.12, bf16[2,2,128,1024]{3,2,1,0:T(8,128)(2,1)S(1)} %get-tuple-element.13), kind=kOutput, calls=%fused_computation.4 | convolution fusion | flops 537395200 | bytes 6815744 | tf_op jit(solution)/shard_map/ejtf,fec->ejtc/dot_general | solution.py:698
  28.1 0.0 copy-done.6
  28.1 152.9 %sublayer.1 = (bf16[256,4096]{1,0:T(8,128)(2,1)S(1)}, bf16[256,4096]{1,0:T(8,128)(2,1)}, bf16[4,256,1024]{2,1,0:T(8,128)(2,1)}) custom-call(s32[4]{0:T(128)S(1)} %copy-done.6, s32[4,2]{1,0:T(4,128)S(1)} %copy.11.lengths_ref, f32[2,2,128,1024]{3,2,1,0:T(8,128)} %fusion.4.part_ref, bf16[256,4096]{1,0:T(8,128)(2,1)} %bitcast.15, bf16[256,4096]{1,0:T(8,128)(2,1)} %bitcast.16), custom_call_target="tpu_custom_call" | custom-call | tf_op jit(solution)/shard_map/sublayer/pallas_call | solution.py:596
  181.0 0.0 copy-start.2
  181.0 1.6 copy-done.2
  182.6 0.0 copy-start.3
  182.6 1.6 copy-done.3
  184.2 3.4 %finish_weight.1 = (f32[8192,128]{1,0:T(8,128)}, bf16[256,4096]{1,0:T(8,128)(2,1)}, bf16[256,4096]{1,0:T(8,128)(2,1)}) custom-call(bf16[2,4,128,512]{3,2,1,0:T(8,128)(2,1)S(1)} %get-tuple-element.12.rows_ref, bf16[4,256,1024]{2,1,0:T(8,128)(2,1)S(1)} %copy-done.3, bf16[256,4096]{1,0:T(8,128)(2,1)S(1)} %get-tuple-element.16.att_ref, ...), custom_call_target="tpu_custom_call" | custom-call | tf_op jit(solution)/shard_map/finish_weight/pallas_call | solution.py:677
Async XLA Ops:
  1.4 1.6 copy-start
  3.0 0.9 copy-start.4
  3.9 0.7 copy-start.5
  24.2 1.6 copy-start.1
  25.8 2.3 %copy-start.6 = (s32[4]{0:T(128)S(1)}, s32[4]{0:T(128)}, u32[]{:S(2)}) copy-start(s32[4]{0:T(128)} %src_ref.3) | copy-start | bytes 52
  181.0 1.6 copy-start.2
  182.6 1.6 copy-start.3

commit v2 on v1

--- a/solution.py
+++ b/solution.py
@@ -15,6 +15,7 @@
 VMEM = pl.BlockSpec(memory_space=pltpu.VMEM)
 SMEM = pl.BlockSpec(memory_space=pltpu.SMEM)
 ANY = pl.BlockSpec(memory_space=pl.ANY)
+HBM = pl.BlockSpec(memory_space=pltpu.HBM)
 DMA = pltpu.SemaphoreType.DMA
 
 
@@ -79,15 +80,19 @@
                 pl.semaphore_wait(barrier, fixed + 1)
 
 
-def text_kernel(dp, ctx, src_ref, own_ref, weight_ref, chosen_ref, rows_ref, other_ref, text,
-                own_sem, w_sems, row_send, row_recv, line_send, line_recv, twin_send, twin_recv):
+def text_kernel(dp, ctx, src_any, own_ref, weight_ref, chosen_ref, rows_ref, pair_ref, src_ref, text,
+                own_sem, src_sem, w_sems, row_send, row_recv, line_send, line_recv, twin_send, twin_recv):
     me = Place(dp, ctx)
     rows, a, b, last = me.rows, me.a, me.b, me.last
     share = ctx // dp
     width = own_ref.shape[2]
     features = share * width
+    load_src = pltpu.make_async_copy(src_any, src_ref, src_sem)
+    load_src.start()
+    weights = remote(weight_ref, pair_ref.at[1], w_sems.at[0], w_sems.at[1], me.twin)
+    own_weights = pltpu.make_async_copy(weight_ref, pair_ref.at[0], w_sems.at[2])
+    own_weights.start()
     me.greet()
-    weights = remote(weight_ref, other_ref, w_sems.at[0], w_sems.at[1], me.twin)
 
     def spot(piece, core):
         return pl.ds(pl.multiple_of((piece + core * share) % (2 * share) * width, width), width)
@@ -167,6 +172,7 @@
     for p in range(2 * share):
         for j in range(rows):
             across(p, j).wait_recv()
+    load_src.wait()
     for b_at in range(dp):
         for e in range(2):
             rows_ref[e, b_at] = text[e, src_ref[b_at], :, pl.ds(0, features)]
@@ -196,6 +202,7 @@
 
             line(i, b, j, 2, me.side).wait_send()
     weights.wait()
+    own_weights.wait()
 
 
 def gather_text(src, own, weight, dp, ctx):
@@ -206,17 +213,19 @@
     pieces = 2 * share
     return pl.pallas_call(
         functools.partial(text_kernel, dp, ctx),
-        in_specs=[SMEM, VMEM, ANY],
-        out_specs=[VMEM, VMEM, ANY],
+        in_specs=[HBM, HBM, HBM],
+        out_specs=[VMEM, VMEM, VMEM],
         out_shape=[
             jax.ShapeDtypeStruct((2, rows, tokens, pieces * width), kind),
             jax.ShapeDtypeStruct((2, dp, tokens, share * width), kind),
-            jax.ShapeDtypeStruct(weight.shape, weight.dtype),
+            jax.ShapeDtypeStruct((2,) + weight.shape, weight.dtype),
         ],
         scratch_shapes=[
+            pltpu.SMEM(src.shape, src.dtype),
             pltpu.VMEM((2, dp, tokens, pieces * width), kind),
             DMA,
-            DMA((2,)),
+            DMA,
+            DMA((3,)),
             DMA,
             DMA((rows,)),
             DMA((pieces, rows, 3)),
@@ -229,8 +238,8 @@
     )(src, own, weight)
 
 
-def sublayer_kernel(dp, ctx, cut, src_ref, lengths_ref, part_ref, q_any, g_any, out_ref, gq_ref, grads_ref,
-                    q_ref, g_ref, sums, kv, gkv, crossed0, risen0, fallen0, going0,
+def sublayer_kernel(dp, ctx, cut, src_any, lengths_any, part_ref, q_any, g_any, out_ref, gq_ref, grads_ref,
+                    src_ref, lengths_ref, q_ref, g_ref, sums, kv, gkv, crossed0, risen0, fallen0, going0,
                     risen1, fallen1, going1, crossed1,
                     in_sems, y_send, y_recv, ag_send, ag_recv, x0_send, x0_recv,
                     up0_send, up0_recv, down0_send, down0_recv,
@@ -245,6 +254,10 @@
     own = me.c
     load_q = pltpu.make_async_copy(q_any, q_ref, in_sems.at[0])
     load_g = pltpu.make_async_copy(g_any, g_ref, in_sems.at[1])
+    load_src = pltpu.make_async_copy(src_any, src_ref, in_sems.at[2])
+    load_lengths = pltpu.make_async_copy(lengths_any, lengths_ref, in_sems.at[3])
+    load_src.start()
+    load_lengths.start()
     load_q.start()
     load_g.start()
     me.greet()
@@ -322,8 +335,10 @@
 
     scale = 1.0 / math.sqrt(HEAD)
     position = lax.broadcasted_iota(jnp.int32, (1, keys), 1)
+    load_src.wait()
+    load_lengths.wait()
     text_at = src_ref[me.d]
-    bound = jnp.where(position < tokens, lengths_ref[text_at, 0], lengths_ref[text_at, 1] + tokens)
+    bound = jnp.where(position < tokens, lengths_ref[0, text_at], lengths_ref[1, text_at] + tokens)
     bias = jnp.where(position < bound, 0.0, -1e30).astype(jnp.float32)
 
     def attend(r, block):
@@ -333,14 +348,14 @@
         key = kv[r, block, :, :HEAD]
         value = kv[r, block, :, HEAD:]
         scores = dot(q, key, ((1,), (1,))) * scale + bias
+        grad_probs = dot(g, value, ((1,), (1,)))
         top = jnp.max(scores, axis=-1, keepdims=True)
         weights = jnp.exp(scores - top)
         probs = weights * (1.0 / jnp.sum(weights, axis=-1, keepdims=True))
         probs_low = probs.astype(jnp.bfloat16)
-        out_ref[:, at] = dot(probs_low, value, ((1,), (0,))).astype(jnp.bfloat16)
-        grad_probs = dot(g, value, ((1,), (1,)))
         delta = jnp.sum(probs * grad_probs, axis=-1, keepdims=True)
         grad_scores = (probs * (grad_probs - delta) * scale).astype(jnp.bfloat16)
+        out_ref[:, at] = dot(probs_low, value, ((1,), (0,))).astype(jnp.bfloat16)
         gq_ref[:, at] = dot(grad_scores, key, ((1,), (0,))).astype(jnp.bfloat16)
         gkv[r, block, :, :HEAD] = dot(grad_scores, q, ((0,), (0,))).astype(gkv.dtype)
         gkv[r, block, :, HEAD:] = dot(probs_low, g, ((0,), (0,))).astype(gkv.dtype)
@@ -408,15 +423,21 @@
         chain0(r, z, rising).start()
 
     def reduce_step(r, s):
-        @pl.when(a == s)
-        def _():
-            for z in range(last, s, -1):
-                pass_on(r, z, True, s == 0)
-
-        @pl.when(a == last - s)
-        def _():
-            for z in range(0, last - s):
-                pass_on(r, z, False, s == 0)
+        @pl.when(a == 0)
+        def _():
+            pass_on(r, last + 1 - s, True, True)
+
+        @pl.when((a > 0) & (a < s))
+        def _():
+            pass_on(r, last + a + 1 - s, True, False)
+
+        @pl.when(a == last)
+        def _():
+            pass_on(r, s - 1, False, True)
+
+        @pl.when((a < last) & (last - a < s))
+        def _():
+            pass_on(r, s - last + a - 1, False, False)
 
     def own_terms(r, low, high, side=None):
         terms = []
@@ -507,40 +528,52 @@
     def _(i):
         for s in range(planes):
 
-            @pl.when(i > 0)
-            def _():
-                reduce_step(i - 1, s)
-
             @pl.when(i < rounds)
             def _():
                 if s == 0:
                     relay_side(i)
                 else:
                     relay(i, s)
-                if s == last:
-
-                    @pl.when(i + 1 < rounds)
-                    def _():
-                        start_round(i + 1)
-
+
+            if s > 0:
+
+                @pl.when(i > 0)
+                def _():
+                    reduce_step(i - 1, s)
+
+            if s == last:
+
+                @pl.when(i + 1 < rounds)
+                def _():
+                    start_round(i + 1)
+
+            if s == min(1, last):
+
+                @pl.when(i > 1)
+                def _():
+                    finish(i - 2)
+
+            if s == min(2, last):
+
+                @pl.when(i > 1)
+                def _():
+                    close(i - 2)
+
+            if s == last:
+
+                @pl.when(i > 2)
+                def _():
+                    spread(i - 3)
+
+            @pl.when(i < rounds)
+            def _():
                 work(i, s)
 
-        @pl.when(i > 1)
-        def _():
-            close(i - 2)
-
-        @pl.when(i > 0)
-        def _():
-            finish(i - 1)
-
         @pl.when(i < rounds)
         def _():
             work(i, planes)
 
-        @pl.when(i > 2)
-        def _():
-            spread(i - 3)
-
+    finish(rounds - 1)
     close(rounds - 1)
     for r in range(max(rounds - 2, 0), rounds):
         spread(r)
@@ -595,7 +628,7 @@
     whole = pltpu.VMEM((rounds, ctx, keys, PAIR), low)
     return pl.pallas_call(
         functools.partial(sublayer_kernel, dp, ctx, cut),
-        in_specs=[SMEM, SMEM, VMEM, ANY, ANY],
+        in_specs=[HBM, HBM, VMEM, HBM, HBM],
         out_specs=[VMEM, VMEM, VMEM],
         out_shape=[
             jax.ShapeDtypeStruct(queries.shape, low),
@@ -603,6 +636,8 @@
             jax.ShapeDtypeStruct((dp, keys, columns), low),
         ],
         scratch_shapes=[
+            pltpu.SMEM(src.shape, src.dtype),
+            pltpu.SMEM(lengths.shape, lengths.dtype),
             pltpu.VMEM(queries.shape, low),
             pltpu.VMEM(queries.shape, low),
             pltpu.VMEM((rounds, rows, 2, tokens, PAIR), jnp.float32),
@@ -616,7 +651,7 @@
             second,
             second,
             pltpu.VMEM((rounds, keys - cut, PAIR), low),
-            DMA((2,)),
+            DMA((4,)),
             DMA((rounds, rows)),
             DMA((rounds, rows)),
             DMA((rounds, 2, ctx, 3)),
@@ -631,7 +666,7 @@
             DMA((rounds, dp)),
             DMA((rounds, rows)),
         ],
-        compiler_params=pltpu.CompilerParams(collective_id=2, has_side_effects=True, vmem_limit_bytes=50 << 20),
+        compiler_params=pltpu.CompilerParams(collective_id=2, has_side_effects=True, vmem_limit_bytes=36 << 20),
         name="sublayer",
     )(src, lengths, part, queries, grad_out)
 
@@ -692,12 +727,11 @@
 
 
 def per_device(dp, ctx, text, src, lengths, kv_weight, queries, grad_out):
-    features = kv_weight.shape[0]
-    chosen, rows, other = gather_text(src, text[0], kv_weight, dp, ctx)
+    chosen, rows, pair = gather_text(src, text[0], kv_weight, dp, ctx)
     dims = "ejtf,fec->ejtc"
-    part = jnp.einsum(dims, chosen[..., :features], kv_weight, preferred_element_type=jnp.float32)
-    part = part + jnp.einsum(dims, chosen[..., features:], other, preferred_element_type=jnp.float32)
-    attended, grad_queries, grads = sublayer(src, lengths, part, queries[0], grad_out[0], dp, ctx)
+    pair = pair.reshape((-1,) + kv_weight.shape[1:])
+    part = jnp.einsum(dims, chosen, pair, preferred_element_type=jnp.float32)
+    attended, grad_queries, grads = sublayer(src, lengths.T, part, queries[0], grad_out[0], dp, ctx)
     attended, grad_queries, weight = finish_weight(rows, grads, attended, grad_queries)
     return (attended[None], grad_queries[None], weight)
 

time: 188 us -> 147 us (0.78)
  Pallas kernels: 176 us -> 141 us
  local copies, waits for them, and re-layouts: 7.78 us -> 3.71 us
    pallas_call x1, Pallas kernels: 153 us -> 119 us  [sublayer(): pl.pallas_call(functools.partial(sublayer_kernel, dp, ctx, cut), in_specs...]
    unnamed x15 -> x14, local copies, waits for them, and re-layouts: 7.78 us -> 3.71 us
where the time goes in v2:
time: 147 us
  Pallas kernels  141 us (96%)
  local copies, waits for them, and re-layouts  3.71 us (3%)
  matrix products  1.62 us (1%)
    pallas_call x1, Pallas kernels, sublayer(): pl.pallas_call(functools.partial(sublayer_kernel, dp, ctx, cut), in_specs...  119 us
    pallas_call x1, Pallas kernels, gather_text(): pl.pallas_call(functools.partial(text_kernel, dp, ctx), in_specs=[HBM, HB...  19.2 us
    unnamed x14, local copies, waits for them, and re-layouts  3.71 us
    pallas_call x1, Pallas kernels, finish_weight(): pl.pallas_call(weight_kernel, in_specs=[VMEM, VMEM, VMEM, VMEM], out_spec...  3.35 us

profile of v2, /device:TPU:0, one launch (start us, length us, event | category | flops | bytes accessed | tf_op | source)
XLA Modules:
  0.0 147.1 jit_solution(11132331326994123580)
XLA Ops:
  0.6 0.0 copy-start
  0.6 1.6 %copy-done = bf16[512,2,1024]{2,1,0:T(2,128)(2,1)S(1)} copy-done((bf16[512,2,1024]{2,1,0:T(2,128)(2,1)S(1)}, bf16[512,2,1024]{2,1,0:T(2,128)(2,1)}, u32[]{:S(2)}) %copy-start) | copy-done | bytes 2097176
  2.2 0.0 copy-start.3
  2.2 0.9 copy-done.3
  3.1 0.0 copy-start.4
  3.1 0.7 copy-done.4
  3.8 19.2 %gather_text.1 = (bf16[2,2,128,1024]{3,2,1,0:T(8,128)(2,1)S(1)}, bf16[2,4,128,512]{3,2,1,0:T(8,128)(2,1)S(1)}, bf16[2,512,2,1024]{3,2,1,0:T(2,128)(2,1)S(1)}) custom-call(s32[4]{0:T(128)S(1)} %copy-done.4, bf16[2,128,256]{2,1,0:T(8,128)(2,1)S(1)} %bitcast.17, bf16[512,2,1024]{2,1,0:T(2,128)(2,1)S(1)} %copy-done), custom_call_target="tpu_custom_call" | custom-call | tf_op jit(solution)/shard_map/gather_text/pallas_call | solution.py:214
  23.0 0.0 copy-start.1
  23.0 0.0 copy-start.2
  23.0 0.0 copy-start.5
  23.0 0.0 copy-start.6
  23.1 1.6 %fusion.part_ref = f32[2,2,128,1024]{3,2,1,0:T(8,128)S(1)} fusion(bf16[2,2,128,1024]{3,2,1,0:T(8,128)(2,1)S(1)} %get-tuple-element.13, bf16[1024,2,1024,1]{2,1,0,3:T(2,128)(2,1)S(1)} %bitcast.19), kind=kOutput, calls=%fused_computation | convolution fusion | flops 1073741824 | bytes 7340032 | tf_op jit(solution)/shard_map/ejtf,fec->ejtc/dot_general | solution.py:733
  24.7 0.0 copy-done.1
  24.7 0.5 copy-done.2
  25.2 0.0 copy-done.5
  25.2 0.0 copy-done.6
  25.2 118.5 %sublayer.1 = (bf16[256,4096]{1,0:T(8,128)(2,1)S(1)}, bf16[256,4096]{1,0:T(8,128)(2,1)S(1)}, bf16[4,256,1024]{2,1,0:T(8,128)(2,1)S(1)}) custom-call(s32[4]{0:T(128)S(1)} %copy-done.5, s32[2,4]{1,0:T(2,128)S(1)} %bitcast.18, f32[2,2,128,1024]{3,2,1,0:T(8,128)S(1)} %fusion.part_ref, bf16[256,4096]{1,0:T(8,128)(2,1)S(1)} %bitcast.15, bf16[256,4096]{1,0:T(8,128)(2,1)S(1)} %bitcast.16), custom_call_target="tpu_custom_call" | custom-call | tf_op jit(solution)/shard_map/sublayer/pallas_call | solution.py:629
  143.7 3.4 %finish_weight.1 = (f32[8192,128]{1,0:T(8,128)}, bf16[256,4096]{1,0:T(8,128)(2,1)}, bf16[256,4096]{1,0:T(8,128)(2,1)}) custom-call(bf16[2,4,128,512]{3,2,1,0:T(8,128)(2,1)S(1)} %get-tuple-element.12.rows_ref, bf16[4,256,1024]{2,1,0:T(8,128)(2,1)S(1)} %get-tuple-element.15.grads_ref, bf16[256,4096]{1,0:T(8,128)(2,1)S(1)} %get-tuple-element.16.att_ref, ...), custom_call_target="tpu_custom_call" | custom-call | tf_op jit(solution)/shard_map/finish_weight/pallas_call | solution.py:712
Async XLA Ops:
  0.6 1.6 %copy-start = (bf16[512,2,1024]{2,1,0:T(2,128)(2,1)S(1)}, bf16[512,2,1024]{2,1,0:T(2,128)(2,1)}, u32[]{:S(2)}) copy-start(bf16[512,2,1024]{2,1,0:T(2,128)(2,1)} %weight_ref.1) | copy-start | bytes 6291460
  2.2 0.9 copy-start.3
  3.1 0.7 copy-start.4
  23.0 1.7 %copy-start.1 = (bf16[1,256,4096]{2,1,0:T(8,128)(2,1)S(1)}, bf16[1,256,4096]{2,1,0:T(8,128)(2,1)}, u32[]{:S(2)}) copy-start(bf16[1,256,4096]{2,1,0:T(8,128)(2,1)} %param.10) | copy-start | bytes 6291460
  23.0 2.2 %copy-start.2 = (bf16[1,256,4096]{2,1,0:T(8,128)(2,1)S(1)}, bf16[1,256,4096]{2,1,0:T(8,128)(2,1)}, u32[]{:S(2)}) copy-start(bf16[1,256,4096]{2,1,0:T(8,128)(2,1)} %param.11) | copy-start | bytes 6291460
  23.0 2.2 %copy-start.5 = (s32[4]{0:T(128)S(1)}, s32[4]{0:T(128)}, u32[]{:S(2)}) copy-start(s32[4]{0:T(128)} %src_any.3) | copy-start | bytes 52
  23.0 2.2 %copy-start.6 = (s32[4,2]{0,1:T(2,128)S(1)}, s32[4,2]{0,1:T(2,128)}, u32[]{:S(2)}) copy-start(s32[4,2]{0,1:T(2,128)} %param.8) | copy-start | bytes 100

commit v3 on v2

--- a/solution.py
+++ b/solution.py
@@ -80,129 +80,159 @@
                 pl.semaphore_wait(barrier, fixed + 1)
 
 
-def text_kernel(dp, ctx, src_any, own_ref, weight_ref, chosen_ref, rows_ref, pair_ref, src_ref, text,
-                own_sem, src_sem, w_sems, row_send, row_recv, line_send, line_recv, twin_send, twin_recv):
+def text_kernel(dp, ctx, src_any, own_ref, weight_ref, chosen_ref, rows_ref, pair_ref, src_ref, text, passing,
+                src_sem, w_sems, line_send, line_recv, row_send, row_recv, side_send, side_recv,
+                twin_send, twin_recv, copy_sems):
     me = Place(dp, ctx)
-    rows, a, b, last = me.rows, me.a, me.b, me.last
+    rows, planes, a, b, last = me.rows, me.planes, me.a, me.b, me.last
     share = ctx // dp
     width = own_ref.shape[2]
     features = share * width
     load_src = pltpu.make_async_copy(src_any, src_ref, src_sem)
     load_src.start()
+    own_weights = pltpu.make_async_copy(weight_ref, pair_ref.at[0], w_sems.at[2])
     weights = remote(weight_ref, pair_ref.at[1], w_sems.at[0], w_sems.at[1], me.twin)
-    own_weights = pltpu.make_async_copy(weight_ref, pair_ref.at[0], w_sems.at[2])
+    me.greet()
+
+    def slot(j, e, piece, core):
+        at = (piece + core * share) % (2 * share) * width
+        return text.at[e, j * 2 + me.core, :, pl.ds(pl.multiple_of(at, width), width)]
+
+    def line(source, z, e, way, target):
+        return remote(source, passing.at[z, e], line_send.at[z, e, way], line_recv.at[z, e], target)
+
+    def to_row(source, z, e, j):
+        row, i = z // share, z % share
+        return remote(source, slot(j, e, i * 2 + b, me.core), row_send.at[z, e], row_recv.at[i, j, e], me.at_row(row))
+
+    def to_side(source, i, j, e):
+        return remote(source, slot(j, e, i * 2 + b, me.core), side_send.at[i, j, e], side_recv.at[i, j, e], me.side)
+
+    def to_twin(source, piece, j, e):
+        return remote(source, slot(j, e, piece, 1 - me.core), twin_send.at[piece, j, e],
+                      twin_recv.at[piece, j, e], me.twin)
+
+    def keep(source, i, e):
+        return pltpu.make_async_copy(source, slot(me.row, e, i * 2 + b, me.core), copy_sems.at[i, e])
+
+    def deliver(source, z, e):
+        i = z % share
+
+        @pl.when(z // share == me.row)
+        def _():
+            to_side(source, i, me.row, e).start()
+            to_twin(source, i * 2 + b, me.row, e).start()
+            keep(source, i, e).start()
+
+        @pl.when(z // share != me.row)
+        def _():
+            to_row(source, z, e, me.row).start()
+
+    def at_distance(s, body):
+        for way in (0, 1) if s else (0,):
+            z = a + s * (2 * way - 1)
+
+            @pl.when((z >= 0) & (z <= last))
+            def _():
+                body(z, 1 - way)
+
+    def arrive(z, way):
+        target = me.up if way == 1 else me.down
+        more = (a < last) if way == 1 else (a > 0)
+        for e in range(2):
+            source = passing.at[z, e]
+            line(source, z, e, 0, me.up).wait_recv()
+
+            @pl.when(more)
+            def _():
+                line(source, z, e, 1 - way, target).start()
+
+            deliver(source, z, e)
+
+    def from_rows(z, way):
+        i = z % share
+
+        @pl.when(z // share == me.row)
+        def _():
+            for j in range(rows):
+
+                @pl.when(me.row != j)
+                def _():
+                    for e in range(2):
+                        source = slot(j, e, i * 2 + b, me.core)
+                        to_row(source, z, e, j).wait_recv()
+                        to_side(source, i, j, e).start()
+                        to_twin(source, i * 2 + b, j, e).start()
+
+    def from_side(z, way):
+        i = z % share
+
+        @pl.when(z // share == me.row)
+        def _():
+            for j_at in range(rows):
+                j = (me.row + j_at) % rows
+                for e in range(2):
+                    to_side(own_ref.at[e], i, j, e).wait_recv()
+                    piece = i * 2 + 1 - b
+                    to_twin(slot(j, e, piece, me.core), piece, j, e).start()
+
+    for e in range(2):
+        source = own_ref.at[e]
+
+        @pl.when(a < last)
+        def _():
+            line(source, a, e, 0, me.up).start()
+
+        @pl.when(a > 0)
+        def _():
+            line(source, a, e, 1, me.down).start()
+
+        deliver(source, a, e)
+    weights.start()
     own_weights.start()
-    me.greet()
-
-    def spot(piece, core):
-        return pl.ds(pl.multiple_of((piece + core * share) % (2 * share) * width, width), width)
-
-    def block(sample, piece, core):
-        return text.at[:, sample, :, spot(piece, core)]
-
-    home = me.c // (2 * share)
-    piece = me.c % (2 * share)
-    mine = pltpu.make_async_copy(own_ref, block(me.d, piece, me.core), own_sem)
-
-    def to_row(row, sample_row):
-        return remote(own_ref, block(sample_row * 2 + me.core, piece, me.core), row_send,
-                      row_recv.at[sample_row], me.at_row(row))
-
-    def line(i, side, j, way, target):
-        p = i * 2 + side
-        where = block(j * 2 + me.core, p, me.core)
-        return remote(where, where, line_send.at[p, j, way], line_recv.at[p, j], target)
-
-    def across(p, j):
-        return remote(block(j * 2 + me.core, p, me.core), block(j * 2 + me.core, p, 1 - me.core),
-                      twin_send.at[p, j], twin_recv.at[p, j], me.twin)
-
-    for row in range(rows):
-
-        @pl.when((home == row) & (me.row != row))
-        def _():
-            to_row(row, me.row).start()
-
-        @pl.when((home == row) & (me.row == row))
-        def _():
-            mine.start()
-
-    weights.start()
-    first = me.row * share
-    high = jnp.where(2 * a >= 2 * first + share, 1, 0)
-    for t in range(share):
-        i = high * (share - 1 - t) + (1 - high) * t
-        plane = first + i
-        for j_at in range(rows):
-            j = (me.row + j_at) % rows
-
-            @pl.when(a == plane)
-            def _():
-                if j_at == 0:
-                    mine.wait()
-                else:
-                    to_row(0, j).wait_recv()
-
-            @pl.when(a > plane)
-            def _():
-                line(i, b, j, 0, me.up).wait_recv()
-
-            @pl.when(a < plane)
-            def _():
-                line(i, b, j, 1, me.down).wait_recv()
-
-            @pl.when((a >= plane) & (a < last))
-            def _():
-                line(i, b, j, 0, me.up).start()
-
-            @pl.when((a <= plane) & (a > 0))
-            def _():
-                line(i, b, j, 1, me.down).start()
-
-            line(i, b, j, 2, me.side).start()
-            across(i * 2 + b, j).start()
-
-    for t in range(share):
-        i = high * (share - 1 - t) + (1 - high) * t
-        for j_at in range(rows):
-            j = (me.row + j_at) % rows
-            line(i, 1 - b, j, 2, me.side).wait_recv()
-            across(i * 2 + 1 - b, j).start()
-
-    for p in range(2 * share):
+    for s in range(1, planes + 2):
+        if s < planes:
+            at_distance(s, arrive)
+        if s <= planes:
+            at_distance(s - 1, from_rows)
+        if s >= 2:
+            at_distance(s - 2, from_side)
+
+    load_src.wait()
+    for i in range(share):
+        for e in range(2):
+            keep(own_ref.at[e], i, e).wait()
+    for piece in range(2 * share):
         for j in range(rows):
-            across(p, j).wait_recv()
-    load_src.wait()
-    for b_at in range(dp):
-        for e in range(2):
+            for e in range(2):
+                to_twin(own_ref.at[e], piece, j, e).wait_recv()
+    for e in range(2):
+        for b_at in range(dp):
             rows_ref[e, b_at] = text[e, src_ref[b_at], :, pl.ds(0, features)]
-    for j in range(rows):
-        for e in range(2):
+        for j in range(rows):
             chosen_ref[e, j] = text[e, src_ref[j * 2 + me.core]]
-    for row in range(rows):
-
-        @pl.when((home == row) & (me.row != row))
-        def _():
-            to_row(row, me.row).wait_send()
-
-    for p in range(2 * share):
-        for j in range(rows):
-            across(p, j).wait_send()
-    for i in range(share):
-        plane = first + i
-        for j in range(rows):
-
-            @pl.when((a >= plane) & (a < last))
-            def _():
-                line(i, b, j, 0, me.up).wait_send()
-
-            @pl.when((a <= plane) & (a > 0))
-            def _():
-                line(i, b, j, 1, me.down).wait_send()
-
-            line(i, b, j, 2, me.side).wait_send()
     weights.wait()
     own_weights.wait()
+    for e in range(2):
+        for piece in range(2 * share):
+            for j in range(rows):
+                to_twin(own_ref.at[e], piece, j, e).wait_send()
+        for i in range(share):
+            for j in range(rows):
+                to_side(own_ref.at[e], i, j, e).wait_send()
+        for z in range(planes):
+
+            @pl.when(z // share != me.row)
+            def _():
+                to_row(own_ref.at[e], z, e, me.row).wait_send()
+
+            @pl.when((a < last) & (z <= a))
+            def _():
+                line(own_ref.at[e], z, e, 0, me.up).wait_send()
+
+            @pl.when((a > 0) & (z >= a))
+            def _():
+                line(own_ref.at[e], z, e, 1, me.down).wait_send()
 
 
 def gather_text(src, own, weight, dp, ctx):
@@ -211,6 +241,7 @@
     rows = dp // 2
     kind = own.dtype
     pieces = 2 * share
+    planes = ctx // 2
     return pl.pallas_call(
         functools.partial(text_kernel, dp, ctx),
         in_specs=[HBM, HBM, HBM],
@@ -223,15 +254,18 @@
         scratch_shapes=[
             pltpu.SMEM(src.shape, src.dtype),
             pltpu.VMEM((2, dp, tokens, pieces * width), kind),
-            DMA,
+            pltpu.VMEM((planes, 2, tokens, width), kind),
             DMA,
             DMA((3,)),
-            DMA,
-            DMA((rows,)),
-            DMA((pieces, rows, 3)),
-            DMA((pieces, rows)),
-            DMA((pieces, rows)),
-            DMA((pieces, rows)),
+            DMA((planes, 2, 2)),
+            DMA((planes, 2)),
+            DMA((planes, 2)),
+            DMA((share, rows, 2)),
+            DMA((share, rows, 2)),
+            DMA((share, rows, 2)),
+            DMA((pieces, rows, 2)),
+            DMA((pieces, rows, 2)),
+            DMA((share, 2)),
         ],
         compiler_params=pltpu.CompilerParams(collective_id=1, has_side_effects=True, vmem_limit_bytes=16 << 20),
         name="gather_text",
@@ -312,26 +346,13 @@
         send_up(r, 1, block)
         send_down(r, 1, block)
 
-    def relay(r, s):
-        @pl.when(a >= s)
-        def _():
-            base = (a - s) * 2
-            ag_wait(r, 0, base + b)
-            send_up(r, 0, base + b)
-            ag(r, 0, base + b, 2, me.side).start()
-            for side in range(2):
-                ag_wait(r, 1, base + side)
-                send_up(r, 1, base + side)
-
-        @pl.when(a + s <= last)
-        def _():
-            base = (a + s) * 2
-            ag_wait(r, 0, base + b)
-            send_down(r, 0, base + b)
-            ag(r, 0, base + b, 2, me.side).start()
-            for side in range(2):
-                ag_wait(r, 1, base + side)
-                send_down(r, 1, base + side)
+    def relay(r, base, send, unit):
+        side = b if unit < 2 else 1 - b
+        part = 0 if unit == 0 else 1
+        ag_wait(r, part, base + side)
+        send(r, part, base + side)
+        if part == 0:
+            ag(r, 0, base + side, 2, me.side).start()
 
     scale = 1.0 / math.sqrt(HEAD)
     position = lax.broadcasted_iota(jnp.int32, (1, keys), 1)
@@ -403,10 +424,11 @@
                 total = total + term[at, :].astype(jnp.float32)
             target[at, :] = total.astype(target.dtype)
 
-    def pass_on(r, z, rising, begins):
+    def pass_on(r, z, rising, begins, unit):
         arrived0 = risen0 if rising else fallen0
         arrived1 = risen1 if rising else fallen1
-        for side in range(2):
+        if unit < 2:
+            side = b if unit == 0 else 1 - b
             source = gkv.at[r, z * 2 + side, parts[1], :]
             if not begins:
                 target = going1.at[r, z, side]
@@ -414,30 +436,39 @@
                 add(target, [source, arrived1.at[r, z, side]])
                 source = target
             chain1(r, z, side, rising, source).start()
-        cross0(r, z).wait_recv()
-        terms = [gkv.at[r, z * 2 + b, parts[0], :], crossed0.at[r, z]]
-        if not begins:
-            chain0(r, z, rising).wait_recv()
-            terms.append(arrived0.at[r, z])
-        add(going0.at[r, z], terms)
-        chain0(r, z, rising).start()
-
-    def reduce_step(r, s):
-        @pl.when(a == 0)
-        def _():
-            pass_on(r, last + 1 - s, True, True)
-
-        @pl.when((a > 0) & (a < s))
-        def _():
-            pass_on(r, last + a + 1 - s, True, False)
-
-        @pl.when(a == last)
-        def _():
-            pass_on(r, s - 1, False, True)
-
-        @pl.when((a < last) & (last - a < s))
-        def _():
-            pass_on(r, s - last + a - 1, False, False)
+        else:
+            cross0(r, z).wait_recv()
+            terms = [gkv.at[r, z * 2 + b, parts[0], :], crossed0.at[r, z]]
+            if not begins:
+                chain0(r, z, rising).wait_recv()
+                terms.append(arrived0.at[r, z])
+            add(going0.at[r, z], terms)
+            chain0(r, z, rising).start()
+
+    def move(i, s, unit):
+        @pl.when((i < rounds) & (a >= s))
+        def _():
+            relay(i, (a - s) * 2, send_up, unit)
+
+        @pl.when((i > 0) & (a == 0))
+        def _():
+            pass_on(i - 1, last + 1 - s, True, True, unit)
+
+        @pl.when((i > 0) & (a > 0) & (a < s))
+        def _():
+            pass_on(i - 1, last + a + 1 - s, True, False, unit)
+
+        @pl.when((i < rounds) & (a + s <= last))
+        def _():
+            relay(i, (a + s) * 2, send_down, unit)
+
+        @pl.when((i > 0) & (a == last))
+        def _():
+            pass_on(i - 1, s - 1, False, True, unit)
+
+        @pl.when((i > 0) & (a < last) & (last - a < s))
+        def _():
+            pass_on(i - 1, s - last + a - 1, False, False, unit)
 
     def own_terms(r, low, high, side=None):
         terms = []
@@ -528,18 +559,15 @@
     def _(i):
         for s in range(planes):
 
-            @pl.when(i < rounds)
-            def _():
-                if s == 0:
+            if s == 0:
+
+                @pl.when(i < rounds)
+                def _():
                     relay_side(i)
-                else:
-                    relay(i, s)
-
-            if s > 0:
-
-                @pl.when(i > 0)
-                def _():
-                    reduce_step(i - 1, s)
+
+            else:
+                for unit in range(3):
+                    move(i, s, unit)
 
             if s == last:
 

time: 147 us -> 137 us (0.932)
  Pallas kernels: 141 us -> 130 us
    pallas_call x1, Pallas kernels: 119 us -> 108 us  [sublayer(): pl.pallas_call(functools.partial(sublayer_kernel, dp, ctx, cut), in_specs...]
where the time goes in v3:
time: 137 us; the launch traced here: 136 us
  Pallas kernels  130 us (95%)
  local copies, waits for them, and re-layouts  3.71 us (3%)
  matrix products  1.62 us (1%)
    pallas_call x1, Pallas kernels, sublayer(): pl.pallas_call(functools.partial(sublayer_kernel, dp, ctx, cut), in_specs...  108 us
    pallas_call x1, Pallas kernels, gather_text(): pl.pallas_call(functools.partial(text_kernel, dp, ctx), in_specs=[HBM, HB...  18.9 us
    unnamed x14, local copies, waits for them, and re-layouts  3.71 us
    pallas_call x1, Pallas kernels, finish_weight(): pl.pallas_call(weight_kernel, in_specs=[VMEM, VMEM, VMEM, VMEM], out_spec...  3.35 us

profile of v3, /device:TPU:0, one launch (start us, length us, event | category | flops | bytes accessed | tf_op | source)
XLA Modules:
  0.0 136.4 jit_solution(8047426493779387763)
XLA Ops:
  0.6 0.0 copy-start
  0.6 1.6 %copy-done = bf16[512,2,1024]{2,1,0:T(2,128)(2,1)S(1)} copy-done((bf16[512,2,1024]{2,1,0:T(2,128)(2,1)S(1)}, bf16[512,2,1024]{2,1,0:T(2,128)(2,1)}, u32[]{:S(2)}) %copy-start) | copy-done | bytes 2097176
  2.2 0.0 copy-start.3
  2.2 0.9 copy-done.3
  3.1 0.0 copy-start.4
  3.1 0.7 copy-done.4
  3.8 18.9 %gather_text.1 = (bf16[2,2,128,1024]{3,2,1,0:T(8,128)(2,1)S(1)}, bf16[2,4,128,512]{3,2,1,0:T(8,128)(2,1)S(1)}, bf16[2,512,2,1024]{3,2,1,0:T(2,128)(2,1)S(1)}) custom-call(s32[4]{0:T(128)S(1)} %copy-done.4, bf16[2,128,256]{2,1,0:T(8,128)(2,1)S(1)} %bitcast.17, bf16[512,2,1024]{2,1,0:T(2,128)(2,1)S(1)} %copy-done), custom_call_target="tpu_custom_call" | custom-call | tf_op jit(solution)/shard_map/gather_text/pallas_call | solution.py:245
  22.7 0.0 copy-start.1
  22.7 0.0 copy-start.2
  22.7 0.0 copy-start.5
  22.7 0.0 copy-start.6
  22.7 1.6 %fusion.part_ref = f32[2,2,128,1024]{3,2,1,0:T(8,128)S(1)} fusion(bf16[2,2,128,1024]{3,2,1,0:T(8,128)(2,1)S(1)} %get-tuple-element.13, bf16[1024,2,1024,1]{2,1,0,3:T(2,128)(2,1)S(1)} %bitcast.19), kind=kOutput, calls=%fused_computation | convolution fusion | flops 1073741824 | bytes 7340032 | tf_op jit(solution)/shard_map/ejtf,fec->ejtc/dot_general | solution.py:761
  24.3 0.0 copy-done.1
  24.3 0.5 copy-done.2
  24.9 0.0 copy-done.5
  24.9 0.0 copy-done.6
  24.9 108.1 %sublayer.1 = (bf16[256,4096]{1,0:T(8,128)(2,1)S(1)}, bf16[256,4096]{1,0:T(8,128)(2,1)S(1)}, bf16[4,256,1024]{2,1,0:T(8,128)(2,1)S(1)}) custom-call(s32[4]{0:T(128)S(1)} %copy-done.5, s32[2,4]{1,0:T(2,128)S(1)} %bitcast.18, f32[2,2,128,1024]{3,2,1,0:T(8,128)S(1)} %fusion.part_ref, bf16[256,4096]{1,0:T(8,128)(2,1)S(1)} %bitcast.15, bf16[256,4096]{1,0:T(8,128)(2,1)S(1)} %bitcast.16), custom_call_target="tpu_custom_call" | custom-call | tf_op jit(solution)/shard_map/sublayer/pallas_call | solution.py:657
  133.0 3.4 %finish_weight.1 = (f32[8192,128]{1,0:T(8,128)}, bf16[256,4096]{1,0:T(8,128)(2,1)}, bf16[256,4096]{1,0:T(8,128)(2,1)}) custom-call(bf16[2,4,128,512]{3,2,1,0:T(8,128)(2,1)S(1)} %get-tuple-element.12.rows_ref, bf16[4,256,1024]{2,1,0:T(8,128)(2,1)S(1)} %get-tuple-element.15.grads_ref, bf16[256,4096]{1,0:T(8,128)(2,1)S(1)} %get-tuple-element.16.att_ref, ...), custom_call_target="tpu_custom_call" | custom-call | tf_op jit(solution)/shard_map/finish_weight/pallas_call | solution.py:740
Async XLA Ops:
  0.6 1.6 %copy-start = (bf16[512,2,1024]{2,1,0:T(2,128)(2,1)S(1)}, bf16[512,2,1024]{2,1,0:T(2,128)(2,1)}, u32[]{:S(2)}) copy-start(bf16[512,2,1024]{2,1,0:T(2,128)(2,1)} %weight_ref.1) | copy-start | bytes 6291460
  2.2 0.9 copy-start.3
  3.1 0.7 copy-start.4
  22.7 1.7 %copy-start.1 = (bf16[1,256,4096]{2,1,0:T(8,128)(2,1)S(1)}, bf16[1,256,4096]{2,1,0:T(8,128)(2,1)}, u32[]{:S(2)}) copy-start(bf16[1,256,4096]{2,1,0:T(8,128)(2,1)} %param.10) | copy-start | bytes 6291460
  22.7 2.2 %copy-start.2 = (bf16[1,256,4096]{2,1,0:T(8,128)(2,1)S(1)}, bf16[1,256,4096]{2,1,0:T(8,128)(2,1)}, u32[]{:S(2)}) copy-start(bf16[1,256,4096]{2,1,0:T(8,128)(2,1)} %param.11) | copy-start | bytes 6291460
  22.7 2.2 %copy-start.5 = (s32[4]{0:T(128)S(1)}, s32[4]{0:T(128)}, u32[]{:S(2)}) copy-start(s32[4]{0:T(128)} %src_any.3) | copy-start | bytes 52
  22.7 2.2 %copy-start.6 = (s32[4,2]{0,1:T(2,128)S(1)}, s32[4,2]{0,1:T(2,128)}, u32[]{:S(2)}) copy-start(s32[4,2]{0,1:T(2,128)} %param.8) | copy-start | bytes 100

commit v4 on v3

--- a/solution.py
+++ b/solution.py
@@ -296,13 +296,28 @@
     load_g.start()
     me.greet()
     parts = (pl.ds(0, cut), pl.ds(cut, keys - cut))
+    pieces = ((1, cut - tokens, tokens), (0, 0, tokens), (1, 0, cut - tokens))
 
     def columns(r):
         return pl.ds(pl.multiple_of(r * PAIR, PAIR), PAIR)
 
-    def partial(r, row, sender):
-        return remote(part_ref.at[:, row, :, columns(r)], sums.at[r, sender], y_send.at[r, row],
-                      y_recv.at[r, sender], me.at_row(row))
+    def partial(r, row, sender, piece):
+        e, low, high = pieces[piece]
+        return remote(part_ref.at[e, row, low:high, columns(r)], sums.at[r, sender, e, low:high, :],
+                      y_send.at[r, row, piece], y_recv.at[r, sender, piece], me.at_row(row))
+
+    def total(r, piece):
+        e, low, high = pieces[piece]
+        for j in range(nrows):
+
+            @pl.when(me.row != j)
+            def _():
+                partial(r, j, j, piece).wait_recv()
+
+        value = part_ref[e, me.row, low:high, columns(r)]
+        for j_at in range(1, nrows):
+            value = value + sums[r, (me.row + j_at) % nrows, e, low:high, :]
+        kv[r, own, e * tokens + low:e * tokens + high, :] = value.astype(kv.dtype)
 
     def ag(r, part, block, way, target):
         where = kv.at[r, block, parts[part], :]
@@ -321,24 +336,20 @@
         def _():
             ag(r, part, block, 1, me.down).start()
 
-    def start_round(r):
-        for j in range(nrows):
-
-            @pl.when(me.row != j)
-            def _():
-                partial(r, j, j).wait_recv()
-
-        for e in range(2):
-            total = part_ref[e, me.row, :, columns(r)]
-            for j_at in range(1, nrows):
-                total = total + sums[r, (me.row + j_at) % nrows, e]
-            kv[r, own, e * tokens:(e + 1) * tokens, :] = total.astype(kv.dtype)
+    def start_round(r, early=False):
+        total(r, 0)
         ag(r, 1, own, 2, me.side).start()
+        if early:
+            send_up(r, 1, own)
+            send_down(r, 1, own)
+        total(r, 1)
+        total(r, 2)
         send_up(r, 0, own)
         send_down(r, 0, own)
         ag(r, 0, own, 2, me.side).start()
-        send_up(r, 1, own)
-        send_down(r, 1, own)
+        if not early:
+            send_up(r, 1, own)
+            send_down(r, 1, own)
 
     def relay_side(r):
         block = a * 2 + 1 - b
@@ -509,14 +520,24 @@
                 [gkv.at[r, own, parts[0], :], crossed0.at[r, a]] + own_terms(r, low, high))
 
         by_place(body)
-
-    def share_grads(r, d, way, target):
-        where = grads_ref.at[d, :, columns(r)]
-        return remote(where, where, dp_send.at[r, way], dp_recv.at[r, d], target)
-
-    def hand_over(r, d):
-        where = grads_ref.at[d, :, columns(r)]
-        return remote(where, where, twin_send.at[r, d // 2], dp_recv.at[r, d], me.twin)
+        publish(r, 0)
+
+    def share_grads(r, part, d, way, target):
+        where = grads_ref.at[d, parts[part], columns(r)]
+        return remote(where, where, dp_send.at[r, part, way], dp_recv.at[r, part, d], target)
+
+    def hand_over(r, part, d):
+        where = grads_ref.at[d, parts[part], columns(r)]
+        return remote(where, where, twin_send.at[r, part, d // 2], dp_recv.at[r, part, d], me.twin)
+
+    def publish(r, part):
+        for j in range(nrows):
+
+            @pl.when(me.row != j)
+            def _():
+                share_grads(r, part, me.d, j, me.at_row(j)).start()
+
+        hand_over(r, part, me.d).start()
 
     def close(r):
         cross1(r).wait_recv()
@@ -526,22 +547,17 @@
                 [gkv.at[r, own, parts[1], :], crossed1.at[r]] + own_terms(r, low, high, b))
 
         by_place(body)
-        for j in range(nrows):
-
-            @pl.when(me.row != j)
-            def _():
-                share_grads(r, me.d, j, me.at_row(j)).start()
-
-        hand_over(r, me.d).start()
+        publish(r, 1)
 
     def spread(r):
-        for j in range(nrows):
-
-            @pl.when(me.row != j)
-            def _():
-                d = j * 2 + me.core
-                share_grads(r, d, j, me.at_row(j)).wait_recv()
-                hand_over(r, d).start()
+        for part in range(2):
+            for j in range(nrows):
+
+                @pl.when(me.row != j)
+                def _():
+                    d = j * 2 + me.core
+                    share_grads(r, part, d, j, me.at_row(j)).wait_recv()
+                    hand_over(r, part, d).start()
 
     @pl.loop(0, rounds)
     def _(r):
@@ -549,9 +565,10 @@
 
             @pl.when(me.row != j)
             def _():
-                partial(r, j, me.row).start()
-
-    start_round(0)
+                for piece in range(3):
+                    partial(r, j, me.row, piece).start()
+
+    start_round(0, True)
     load_q.wait()
     load_g.wait()
 
@@ -609,13 +626,16 @@
     @pl.loop(0, rounds)
     def _(r):
         for j in range(nrows):
-            hand_over(r, j * 2 + 1 - me.core).wait_recv()
-            hand_over(r, j * 2 + me.core).wait_send()
+            for part in range(2):
+                hand_over(r, part, j * 2 + 1 - me.core).wait_recv()
+                hand_over(r, part, j * 2 + me.core).wait_send()
 
             @pl.when(me.row != j)
             def _():
-                partial(r, j, me.row).wait_send()
-                share_grads(r, me.d, j, me.at_row(j)).wait_send()
+                for piece in range(3):
+                    partial(r, j, me.row, piece).wait_send()
+                for part in range(2):
+                    share_grads(r, part, me.d, j, me.at_row(j)).wait_send()
 
         ag(r, 1, own, 2, me.side).wait_send()
         cross1(r).wait_send()
@@ -680,8 +700,8 @@
             second,
             pltpu.VMEM((rounds, keys - cut, PAIR), low),
             DMA((4,)),
-            DMA((rounds, rows)),
-            DMA((rounds, rows)),
+            DMA((rounds, rows, 3)),
+            DMA((rounds, rows, 3)),
             DMA((rounds, 2, ctx, 3)),
             DMA((rounds, 2, ctx)),
         ]
@@ -690,11 +710,11 @@
         + [
             DMA((rounds,)),
             DMA((rounds,)),
-            DMA((rounds, rows)),
-            DMA((rounds, dp)),
-            DMA((rounds, rows)),
+            DMA((rounds, 2, rows)),
+            DMA((rounds, 2, dp)),
+            DMA((rounds, 2, rows)),
         ],
-        compiler_params=pltpu.CompilerParams(collective_id=2, has_side_effects=True, vmem_limit_bytes=36 << 20),
+        compiler_params=pltpu.CompilerParams(collective_id=2, has_side_effects=True, vmem_limit_bytes=44 << 20),
         name="sublayer",
     )(src, lengths, part, queries, grad_out)
 

time: 137 us -> 136 us (level)
    unnamed x14 -> x10, local copies, waits for them, and re-layouts: 3.71 us -> 3.16 us
where the time goes in v4:
time: 136 us; the launch traced here: 135 us
  Pallas kernels  130 us (96%)
  local copies, waits for them, and re-layouts  3.16 us (2%)
  matrix products  1.62 us (1%)
    pallas_call x1, Pallas kernels, sublayer(): pl.pallas_call(functools.partial(sublayer_kernel, dp, ctx, cut), in_specs...  108 us
    pallas_call x1, Pallas kernels, gather_text(): pl.pallas_call(functools.partial(text_kernel, dp, ctx), in_specs=[HBM, HB...  18.9 us
    pallas_call x1, Pallas kernels, finish_weight(): pl.pallas_call(weight_kernel, in_specs=[VMEM, VMEM, VMEM, VMEM], out_spec...  3.35 us
    unnamed x10, local copies, waits for them, and re-layouts  3.16 us

profile of v4, /device:TPU:0, one launch (start us, length us, event | category | flops | bytes accessed | tf_op | source)
XLA Modules:
  0.0 135.4 jit_solution(15289889043018458621)
XLA Ops:
  0.6 0.0 copy-start
  0.6 1.6 %copy-done = bf16[512,2,1024]{2,1,0:T(2,128)(2,1)S(1)} copy-done((bf16[512,2,1024]{2,1,0:T(2,128)(2,1)S(1)}, bf16[512,2,1024]{2,1,0:T(2,128)(2,1)}, u32[]{:S(2)}) %copy-start) | copy-done | bytes 2097176
  2.2 0.0 copy-start.1
  2.2 0.9 copy-done.1
  3.1 0.0 copy-start.2
  3.1 0.7 copy-done.2
  3.8 18.9 %gather_text.1 = (bf16[2,2,128,1024]{3,2,1,0:T(8,128)(2,1)S(1)}, bf16[2,4,128,512]{3,2,1,0:T(8,128)(2,1)S(1)}, bf16[2,512,2,1024]{3,2,1,0:T(2,128)(2,1)S(1)}) custom-call(s32[4]{0:T(128)S(1)} %copy-done.2, bf16[2,128,256]{2,1,0:T(8,128)(2,1)S(1)} %bitcast.15, bf16[512,2,1024]{2,1,0:T(2,128)(2,1)S(1)} %copy-done), custom_call_target="tpu_custom_call" | custom-call | tf_op jit(solution)/shard_map/gather_text/pallas_call | solution.py:245
  22.7 0.0 copy-start.3
  22.7 0.0 copy-start.4
  22.7 1.6 %fusion.part_ref = f32[2,2,128,1024]{3,2,1,0:T(8,128)S(1)} fusion(bf16[2,2,128,1024]{3,2,1,0:T(8,128)(2,1)S(1)} %get-tuple-element.13, bf16[1024,2,1024,1]{2,1,0,3:T(2,128)(2,1)S(1)} %bitcast.17), kind=kOutput, calls=%fused_computation | convolution fusion | flops 1073741824 | bytes 7340032 | tf_op jit(solution)/shard_map/ejtf,fec->ejtc/dot_general | solution.py:781
  24.3 0.0 copy-done.3
  24.3 0.0 copy-done.4
  24.3 107.6 %sublayer.1 = (bf16[256,4096]{1,0:T(8,128)(2,1)S(1)}, bf16[256,4096]{1,0:T(8,128)(2,1)S(1)}, bf16[4,256,1024]{2,1,0:T(8,128)(2,1)S(1)}) custom-call(s32[4]{0:T(128)S(1)} %copy-done.3, s32[2,4]{1,0:T(2,128)S(1)} %bitcast.16, f32[2,2,128,1024]{3,2,1,0:T(8,128)S(1)} %fusion.part_ref, bf16[256,4096]{1,0:T(8,128)(2,1)} %bitcast.18, bf16[256,4096]{1,0:T(8,128)(2,1)} %bitcast.19), custom_call_target="tpu_custom_call" | custom-call | tf_op jit(solution)/shard_map/sublayer/pallas_call | solution.py:677
  131.9 3.4 %finish_weight.1 = (f32[8192,128]{1,0:T(8,128)}, bf16[256,4096]{1,0:T(8,128)(2,1)}, bf16[256,4096]{1,0:T(8,128)(2,1)}) custom-call(bf16[2,4,128,512]{3,2,1,0:T(8,128)(2,1)S(1)} %get-tuple-element.12.rows_ref, bf16[4,256,1024]{2,1,0:T(8,128)(2,1)S(1)} %get-tuple-element.15.grads_ref, bf16[256,4096]{1,0:T(8,128)(2,1)S(1)} %get-tuple-element.16.att_ref, ...), custom_call_target="tpu_custom_call" | custom-call | tf_op jit(solution)/shard_map/finish_weight/pallas_call | solution.py:760
Async XLA Ops:
  0.6 1.6 %copy-start = (bf16[512,2,1024]{2,1,0:T(2,128)(2,1)S(1)}, bf16[512,2,1024]{2,1,0:T(2,128)(2,1)}, u32[]{:S(2)}) copy-start(bf16[512,2,1024]{2,1,0:T(2,128)(2,1)} %weight_ref.1) | copy-start | bytes 6291460
  2.2 0.9 copy-start.1
  3.1 0.7 copy-start.2
  22.7 1.7 %copy-start.3 = (s32[4]{0:T(128)S(1)}, s32[4]{0:T(128)}, u32[]{:S(2)}) copy-start(s32[4]{0:T(128)} %src_any.3) | copy-start | bytes 52
  22.7 1.7 %copy-start.4 = (s32[4,2]{0,1:T(2,128)S(1)}, s32[4,2]{0,1:T(2,128)}, u32[]{:S(2)}) copy-start(s32[4,2]{0,1:T(2,128)} %param.8) | copy-start | bytes 100

commit v5 on v4

--- a/solution.py
+++ b/solution.py
@@ -80,14 +80,13 @@
                 pl.semaphore_wait(barrier, fixed + 1)
 
 
-def text_kernel(dp, ctx, src_any, own_ref, weight_ref, chosen_ref, rows_ref, pair_ref, src_ref, text, passing,
+def text_kernel(dp, ctx, src_any, own_ref, weight_ref, chosen_ref, text, pair_ref, src_ref, passing,
                 src_sem, w_sems, line_send, line_recv, row_send, row_recv, side_send, side_recv,
                 twin_send, twin_recv, copy_sems):
     me = Place(dp, ctx)
     rows, planes, a, b, last = me.rows, me.planes, me.a, me.b, me.last
     share = ctx // dp
     width = own_ref.shape[2]
-    features = share * width
     load_src = pltpu.make_async_copy(src_any, src_ref, src_sem)
     load_src.start()
     own_weights = pltpu.make_async_copy(weight_ref, pair_ref.at[0], w_sems.at[2])
@@ -207,8 +206,6 @@
             for e in range(2):
                 to_twin(own_ref.at[e], piece, j, e).wait_recv()
     for e in range(2):
-        for b_at in range(dp):
-            rows_ref[e, b_at] = text[e, src_ref[b_at], :, pl.ds(0, features)]
         for j in range(rows):
             chosen_ref[e, j] = text[e, src_ref[j * 2 + me.core]]
     weights.wait()
@@ -248,12 +245,11 @@
         out_specs=[VMEM, VMEM, VMEM],
         out_shape=[
             jax.ShapeDtypeStruct((2, rows, tokens, pieces * width), kind),
-            jax.ShapeDtypeStruct((2, dp, tokens, share * width), kind),
+            jax.ShapeDtypeStruct((2, dp, tokens, pieces * width), kind),
             jax.ShapeDtypeStruct((2,) + weight.shape, weight.dtype),
         ],
         scratch_shapes=[
             pltpu.SMEM(src.shape, src.dtype),
-            pltpu.VMEM((2, dp, tokens, pieces * width), kind),
             pltpu.VMEM((planes, 2, tokens, width), kind),
             DMA,
             DMA((3,)),
@@ -719,14 +715,14 @@
     )(src, lengths, part, queries, grad_out)
 
 
-def weight_kernel(rows_ref, grads_ref, att_ref, gq_ref, out_ref, att_out, gq_out, buffer, sems):
+def weight_kernel(src_ref, rows_ref, grads_ref, att_ref, gq_ref, out_ref, att_out, gq_out, buffer, sems):
     keep_att = pltpu.make_async_copy(att_ref, att_out, sems.at[0])
     keep_gq = pltpu.make_async_copy(gq_ref, gq_out, sems.at[1])
     keep_att.start()
     keep_gq.start()
     dp, keys, columns = grads_ref.shape
     tokens = keys // 2
-    features = rows_ref.shape[3]
+    features = rows_ref.shape[3] // 2
     lanes = columns // HEAD
     stride = 2 * lanes
     size = HEAD
@@ -737,7 +733,9 @@
 
     for i in range(features // size):
         for e in range(2):
-            left = rows_ref[e, :, :, i * size:(i + 1) * size].reshape(dp * tokens, size)
+            left = jnp.concatenate(
+                [rows_ref[e, src_ref[at], :, i * size:(i + 1) * size] for at in range(dp)], axis=0
+            )
             for j in range(columns // PAIR):
                 right = grads_ref[:, e * tokens:(e + 1) * tokens, j * PAIR:(j + 1) * PAIR].reshape(dp * tokens, PAIR)
                 block = dot(left, right, ((0,), (0,)))
@@ -752,14 +750,14 @@
     keep_gq.wait()
 
 
-def finish_weight(rows, grads, attended, grad_queries):
+def finish_weight(src, rows, grads, attended, grad_queries):
     dp, keys, columns = grads.shape
-    features = rows.shape[3]
+    features = rows.shape[3] // 2
     lanes = columns // HEAD
     flat = (features * lanes * 2, HEAD)
     weight, attended, grad_queries = pl.pallas_call(
         weight_kernel,
-        in_specs=[VMEM, VMEM, VMEM, VMEM],
+        in_specs=[SMEM, VMEM, VMEM, VMEM, VMEM],
         out_specs=[ANY, ANY, ANY],
         out_shape=[
             jax.ShapeDtypeStruct(flat, jnp.float32),
@@ -769,7 +767,7 @@
         scratch_shapes=[pltpu.VMEM(flat, jnp.float32), DMA((2 + features // HEAD,))],
         compiler_params=pltpu.CompilerParams(vmem_limit_bytes=24 << 20),
         name="finish_weight",
-    )(rows, grads, attended, grad_queries)
+    )(src, rows, grads, attended, grad_queries)
     weight = weight.reshape(features, lanes, 2, HEAD).transpose(0, 2, 1, 3).reshape(features, 2, columns)
     return attended, grad_queries, weight
 
@@ -780,7 +778,7 @@
     pair = pair.reshape((-1,) + kv_weight.shape[1:])
     part = jnp.einsum(dims, chosen, pair, preferred_element_type=jnp.float32)
     attended, grad_queries, grads = sublayer(src, lengths.T, part, queries[0], grad_out[0], dp, ctx)
-    attended, grad_queries, weight = finish_weight(rows, grads, attended, grad_queries)
+    attended, grad_queries, weight = finish_weight(src, rows, grads, attended, grad_queries)
     return (attended[None], grad_queries[None], weight)
 
 

time: 136 us -> 136 us (level)
  no operation moved by 1% of the time
where the time goes in v5:
time: 136 us; the launch traced here: 135 us
  Pallas kernels  130 us (96%)
  local copies, waits for them, and re-layouts  3.16 us (2%)
  matrix products  1.62 us (1%)
    pallas_call x1, Pallas kernels, sublayer(): pl.pallas_call(functools.partial(sublayer_kernel, dp, ctx, cut), in_specs...  107 us
    pallas_call x1, Pallas kernels, gather_text(): pl.pallas_call(functools.partial(text_kernel, dp, ctx), in_specs=[HBM, HB...  18.9 us
    pallas_call x1, Pallas kernels, finish_weight(): pl.pallas_call(weight_kernel, in_specs=[SMEM, VMEM, VMEM, VMEM, VMEM], ou...  4.25 us
    unnamed x10, local copies, waits for them, and re-layouts  3.16 us

profile of v5, /device:TPU:0, one launch (start us, length us, event | category | flops | bytes accessed | tf_op | source)
XLA Modules:
  0.0 135.4 jit_solution(6709320049533440300)
XLA Ops:
  0.6 0.0 copy-start
  0.6 1.6 %copy-done = bf16[512,2,1024]{2,1,0:T(2,128)(2,1)S(1)} copy-done((bf16[512,2,1024]{2,1,0:T(2,128)(2,1)S(1)}, bf16[512,2,1024]{2,1,0:T(2,128)(2,1)}, u32[]{:S(2)}) %copy-start) | copy-done | bytes 2097176
  2.2 0.0 copy-start.1
  2.2 0.9 copy-done.1
  3.1 0.0 copy-start.2
  3.1 0.7 copy-done.2
  3.8 18.9 %gather_text.1 = (bf16[2,2,128,1024]{3,2,1,0:T(8,128)(2,1)S(1)}, bf16[2,4,128,1024]{3,2,1,0:T(8,128)(2,1)S(1)}, bf16[2,512,2,1024]{3,2,1,0:T(2,128)(2,1)S(1)}) custom-call(s32[4]{0:T(128)S(1)} %copy-done.2, bf16[2,128,256]{2,1,0:T(8,128)(2,1)S(1)} %bitcast.15, bf16[512,2,1024]{2,1,0:T(2,128)(2,1)S(1)} %copy-done), custom_call_target="tpu_custom_call" | custom-call | tf_op jit(solution)/shard_map/gather_text/pallas_call | solution.py:242
  22.7 0.0 copy-start.3
  22.7 0.0 copy-start.4
  22.7 1.6 %fusion.part_ref = f32[2,2,128,1024]{3,2,1,0:T(8,128)S(1)} fusion(bf16[2,2,128,1024]{3,2,1,0:T(8,128)(2,1)S(1)} %get-tuple-element.13, bf16[1024,2,1024,1]{2,1,0,3:T(2,128)(2,1)S(1)} %bitcast.17), kind=kOutput, calls=%fused_computation | convolution fusion | flops 1073741824 | bytes 7340032 | tf_op jit(solution)/shard_map/ejtf,fec->ejtc/dot_general | solution.py:779
  24.3 0.0 copy-done.3
  24.3 0.0 copy-done.4
  24.3 106.7 %sublayer.1 = (bf16[256,4096]{1,0:T(8,128)(2,1)S(1)}, bf16[256,4096]{1,0:T(8,128)(2,1)S(1)}, bf16[4,256,1024]{2,1,0:T(8,128)(2,1)S(1)}) custom-call(s32[4]{0:T(128)S(1)} %copy-done.3, s32[2,4]{1,0:T(2,128)S(1)} %bitcast.16, f32[2,2,128,1024]{3,2,1,0:T(8,128)S(1)} %fusion.part_ref, bf16[256,4096]{1,0:T(8,128)(2,1)} %bitcast.18, bf16[256,4096]{1,0:T(8,128)(2,1)} %bitcast.19), custom_call_target="tpu_custom_call" | custom-call | tf_op jit(solution)/shard_map/sublayer/pallas_call | solution.py:673
  131.0 4.3 %finish_weight.1 = (f32[8192,128]{1,0:T(8,128)}, bf16[256,4096]{1,0:T(8,128)(2,1)}, bf16[256,4096]{1,0:T(8,128)(2,1)}) custom-call(s32[4]{0:T(128)S(1)} %copy-done.3, bf16[2,4,128,1024]{3,2,1,0:T(8,128)(2,1)S(1)} %get-tuple-element.12.rows_ref, bf16[4,256,1024]{2,1,0:T(8,128)(2,1)S(1)} %get-tuple-element.15.grads_ref, ...), custom_call_target="tpu_custom_call" | custom-call | tf_op jit(solution)/shard_map/finish_weight/pallas_call | solution.py:758
Async XLA Ops:
  0.6 1.6 %copy-start = (bf16[512,2,1024]{2,1,0:T(2,128)(2,1)S(1)}, bf16[512,2,1024]{2,1,0:T(2,128)(2,1)}, u32[]{:S(2)}) copy-start(bf16[512,2,1024]{2,1,0:T(2,128)(2,1)} %weight_ref.1) | copy-start | bytes 6291460
  2.2 0.9 copy-start.1
  3.1 0.7 copy-start.2
  22.7 1.7 %copy-start.3 = (s32[4]{0:T(128)S(1)}, s32[4]{0:T(128)}, u32[]{:S(2)}) copy-start(s32[4]{0:T(128)} %src_ref.1) | copy-start | bytes 52
  22.7 1.7 %copy-start.4 = (s32[4,2]{0,1:T(2,128)S(1)}, s32[4,2]{0,1:T(2,128)}, u32[]{:S(2)}) copy-start(s32[4,2]{0,1:T(2,128)} %param.8) | copy-start | bytes 100
